TPU v7x, 32 devices: a whole 2x2x4 slice. The times are simulated.
32 devices in a mesh: px: 4 (over z), py: 4 (over y, x), pz: 2 (over core).
Axes of the slice: x: 2, y: 2, z: 4, core: 2. Of those that a mesh axis runs over, the one named last changes fastest.
Arguments:
- right_side: float32 [16, 64, 256], P('px', 'py', 'pz'), may hold values from -160 to 160
- start_guess: float32 [16, 64, 256], P('px', 'py', 'pz'), may hold values from -4 to 4
- conductivity: float32 [16, 64, 256], P('px', 'py', 'pz'), may hold values from 0.05 to 0.4
- recycled: float32 [16, 16, 64, 256], P(None, 'px', 'py', 'pz'), may hold values from -6 to 6
Outputs:
- solution: float32 [16, 64, 256], P('px', 'py', 'pz')
- residual: float32 [16, 64, 256], P('px', 'py', 'pz')
- hessenberg: float32 [9, 8], replicated
All inputs are finite; a program needn't handle non-finite values.
Results may differ from a plain program's by a relative error of at most 0.03.
Values sent between devices are 32-bit elements; how exact they have to be, the bound alone decides.
A program may use at most 128 MiB of HBM per device.

v0:
```python
import functools
import itertools

import jax
import jax.numpy as jnp
from jax import lax
from jax.experimental import pallas as pl
from jax.experimental.pallas import tpu as pltpu
from jax.sharding import PartitionSpec as P

STEPS = 8
MESH = pl.DeviceIdType.MESH
AXES = ("px", "py", "pz")
TWO = (("py", "pz"), ("px",))
ONE = (("px", "py", "pz"),)
CHUNK = 8

edge_weight = 0.25 ** (1.0 / 3.0)
middle_weight = 2.0 * edge_weight
shift_value = 0.4

DIRS = [d for d in itertools.product((-1, 0, 1), repeat=3) if d != (0, 0, 0)]


def kernel(
    sizes, groups,
    rhs, guess, cond, rec,
    sol_out, res_out, hes_out,
    src, img, bface, bedge, pack, pface, pedge,
    bx, by, bc,
    zm, zx, zy, zc,
    mx, my, mc,
    wbuf, wface, wedge,
    fields, kext, diag, temp, zext,
    gpart, gred1, gred2, sred1, sred2,
    mat, hcols, scale, coef, ecoef,
    hsend, hrecv, rsend, rrecv,
):
    nsz = dict(zip(AXES, sizes))
    me = {a: lax.axis_index(a) for a in AXES}
    K, X, Y, Z = rec.shape
    NF = K + 2
    C0 = K
    f32 = jnp.float32
    lane3 = lax.broadcasted_iota(jnp.int32, (X + 2, Y + 8, Z), 2)
    lane2 = lax.broadcasted_iota(jnp.int32, (32, Z), 1)
    row2 = lax.broadcasted_iota(jnp.int32, (32, Z), 0)

    def exists(d):
        ok = None
        for a, s in zip(AXES, d):
            if s == 0:
                continue
            here = (me[a] < nsz[a] - 1) if s > 0 else (me[a] > 0)
            ok = here if ok is None else jnp.logical_and(ok, here)
        return ok

    def possible(d):
        return all(s == 0 or nsz[a] > 1 for a, s in zip(AXES, d))

    dirs = [(i, d) for i, d in enumerate(DIRS) if possible(d)]

    def target(d):
        return tuple(me[a] + s for a, s in zip(AXES, d))

    def group_info(group):
        n = 1
        rank = 0
        for a in group:
            n *= nsz[a]
            rank = rank * nsz[a] + me[a]
        return n, rank

    def member(group, r):
        co = dict(me)
        for a in reversed(group):
            co[a] = lax.rem(r, nsz[a])
            r = lax.div(r, nsz[a])
        return tuple(co[a] for a in AXES)

    def copies(sends, recvs, slot, zones):
        out = []
        for i, (dx, dy, dz) in dirs:
            if (dz != 0) not in zones:
                continue
            main, face, edge = sends(dz)
            rm, rx, ry, rc = recvs(-dz)
            hx, hy = int(dx > 0), int(dy > 0)
            if dx == 0 and dy == 0:
                s, t = main, rm
            elif dy == 0:
                s, t = main.at[:, X - 1 if hx else 0], rx.at[1 - hx]
            elif dx == 0:
                s, t = face.at[hy], ry.at[1 - hy]
            else:
                s, t = edge.at[hx, hy], rc.at[1 - hx, 1 - hy]
            d = (dx, dy, dz)
            out.append((d, pltpu.make_async_remote_copy(
                src_ref=s, dst_ref=t,
                send_sem=hsend.at[slot, i], recv_sem=hrecv.at[slot, i],
                device_id=target(d), device_id_type=MESH,
            )))
        return out

    def start_halo(cs):
        for d, c in cs:
            pl.when(exists(d))(c.start)

    def wait_recv(cs):
        for d, c in cs:
            pl.when(exists(tuple(-s for s in d)))(c.wait_recv)

    def wait_send(cs):
        for d, c in cs:
            pl.when(exists(d))(c.wait_send)

    NC = (NF + CHUNK - 1) // CHUNK

    def batch_copies(b, c):
        f0, f1 = c * CHUNK, min((c + 1) * CHUNK, NF)
        fs, es = pl.ds(f0, f1 - f0), pl.ds(f0, CHUNK)
        rows = pl.ds(f0 * X, min(CHUNK * X, bface.shape[2] - f0 * X))

        def sends(dz):
            if dz == 0:
                body = (src if b == 0 else img).at[fs]
                return body, bface.at[b, :, rows], bedge.at[b, :, :, es]
            h = int(dz > 0)
            return pack.at[b, h], pface.at[b, h], pedge.at[b, h]

        def recvs(z):
            if z == 0:
                return None, bx.at[b, :, fs], by.at[b, :, rows], bc.at[b, :, :, es]
            h = int(z > 0)
            return zm.at[b, h], zx.at[b, h], zy.at[b, h], zc.at[b, h]

        return copies(sends, recvs, b * (NC + 1) + c, (c == NC,))

    def step_copies(par):
        def sends(dz):
            return wbuf.at[par], wface.at[par], wedge.at[par]

        def recvs(z):
            if z == 0:
                return None, mx.at[par], my.at[par], mc.at[par]
            h = int(z > 0)
            return zm.at[2 + par, h], zx.at[2 + par, h], zy.at[2 + par, h], zc.at[2 + par, h]

        return copies(sends, recvs, 2 * (NC + 1) + par, (False, True))

    def pack_faces(val, face, edge, row, erow):
        for h, y in ((0, 0), (1, Y - 1)):
            for x in range(X):
                face[h, pl.ds(row + x, 1), :] = val[x, y : y + 1, :]
            edge[0, h, pl.ds(erow, 1), :] = val[0, y : y + 1, :]
            edge[1, h, pl.ds(erow, 1), :] = val[X - 1, y : y + 1, :]

    def assemble(dst, main, rx, ry, rc, f, row, erow):
        dst[1 : X + 1, 0:Y, :] = main
        dst[0, 0:Y, :] = rx[0, f]
        dst[X + 1, 0:Y, :] = rx[1, f]
        for h, y in ((1, Y), (0, Y + 7)):
            for x in range(X):
                dst[1 + x, y : y + 1, :] = ry[h, pl.ds(row + x, 1), :]
            dst[0, y : y + 1, :] = rc[0, h, pl.ds(erow, 1), :]
            dst[X + 1, y : y + 1, :] = rc[1, h, pl.ds(erow, 1), :]

    def assemble_zones(slot):
        for h in range(2):
            assemble(zext.at[h], zm[slot, h, 0], zx.at[slot, h], zy.at[slot, h], zc.at[slot, h], 0, 0, 0)

    def zone_field(f):
        low = pltpu.roll(zext[0], lax.rem(2 * Z - 1 - f, Z), 2)
        high = pltpu.roll(zext[1], lax.rem(Z - f, Z), 2)
        return jnp.where(lane3 == Z - 1, low, jnp.where(lane3 == 0, high, 0.0))

    def pack_lanes(get, count, b):
        lane = lax.broadcasted_iota(jnp.int32, (X, Y, Z), 2)
        low = jnp.zeros((X, Y, Z), f32)
        high = jnp.zeros((X, Y, Z), f32)
        for f in range(count):
            v = get(f)
            low = jnp.where(lane == f, pltpu.roll(v, f, 2) if f else v, low)
            high = jnp.where(lane == f, pltpu.roll(v, (f + 1) % Z, 2), high)
        for h, v in ((0, low), (1, high)):
            pack[b, h, 0] = v
            pack_faces(v, pface.at[b, h], pedge.at[b, h], 0, 0)

    def stencil(e, b):
        left = pltpu.roll(jnp.where(lane3 == Z - 1, b, e), 1, 2)
        right = pltpu.roll(jnp.where(lane3 == 0, b, e), Z - 1, 2)
        az = edge_weight * (left + right) + middle_weight * e
        ay = edge_weight * (pltpu.roll(az, 1, 1) + pltpu.roll(az, Y + 7, 1)) + middle_weight * az
        ay = ay[:, :Y]
        ax = edge_weight * (ay[:X] + ay[2:]) + middle_weight * ay[1 : X + 1]
        return ax - 2.0 * e[1 : X + 1, :Y]

    def apply(e, b):
        k = kext[0]
        near = stencil(e, b)
        far = stencil(k * e, kext[1] * b)
        return diag[...] * e[1 : X + 1, :Y] - 0.5 * k[1 : X + 1, :Y] * near - 0.5 * far

    def tile_sum(v):
        v = jnp.sum(v.reshape(X * Y // 8, 8, Z), axis=0)
        return jnp.sum(v, axis=0, keepdims=True)

    def all_reduce(value, groups, bufs, slot, between):
        total = value
        for g, group in enumerate(groups):
            n, rank = group_info(group)
            buf = bufs[g]
            buf[rank] = total
            cs = []
            for k in sorted(range(1, n), key=lambda k: -min(k, n - k)):
                c = pltpu.make_async_remote_copy(
                    src_ref=buf.at[rank], dst_ref=buf.at[rank],
                    send_sem=rsend.at[slot, g, k], recv_sem=rrecv.at[slot, g, k],
                    device_id=member(group, lax.rem(rank + k, n)), device_id_type=MESH,
                )
                c.start()
                cs.append((k, c))
            if g == len(groups) - 1:
                between()
            for k, c in cs:
                pltpu.make_async_remote_copy(
                    src_ref=buf.at[rank], dst_ref=buf.at[lax.rem(rank + n - k, n)],
                    send_sem=rsend.at[slot, g, k], recv_sem=rrecv.at[slot, g, k],
                    device_id=member(group, lax.rem(rank + k, n)), device_id_type=MESH,
                ).wait_recv()
            parts = [buf[r] for r in range(n)]
            while len(parts) > 1:
                parts = [sum(parts[r : r + 2][1:], parts[r]) for r in range(0, len(parts), 2)]
            total = parts[0]
            for k, c in cs:
                c.wait_send()
        return total

    def clear_all(refs):
        for ref in refs:
            def clear(i, carry, ref=ref):
                ref[i] = jnp.zeros(ref.shape[1:], f32)
                return carry

            lax.fori_loop(0, ref.shape[0], clear, 0)

    clear_all((bx, by, bc, zm, zx, zy, zc, mx, my, mc))
    barrier = pltpu.get_barrier_semaphore()
    count = jnp.int32(0)
    for group in ONE:
        n, rank = group_info(group)
        for k in range(1, n):
            pl.semaphore_signal(
                barrier, inc=1, device_id=member(group, lax.rem(rank + k, n)), device_id_type=MESH
            )
        count = count + (n - 1)

    clear_all((wface, wedge, bface, bedge, pface, pedge))

    def load_field(f, carry):
        v = rec[f]
        src[f] = v
        pack_faces(v, bface.at[0], bedge.at[0], f * X, f)
        return carry

    lax.fori_loop(0, K, load_field, 0)
    for f, ref in ((K, guess), (K + 1, cond)):
        v = ref[...]
        src[f] = v
        pack_faces(v, bface.at[0], bedge.at[0], f * X, f)
    pack_lanes(lambda f: src[f], NF, 0)
    pl.semaphore_wait(barrier, count)

    first = [batch_copies(0, c) for c in range(NC + 1)]
    second = [batch_copies(1, c) for c in range(NC + 1)]
    order = [NC - 1] + list(range(NC - 1))
    for c in [NC] + order:
        start_halo(first[c])
    clear_all((fields, kext, zext))
    temp[...] = jnp.zeros(temp.shape, f32)
    img[NF - 1] = jnp.zeros((X, Y, Z), f32)
    wait_recv(first[NC])
    assemble_zones(0)

    def image(f, carry):
        assemble(temp, src[f], bx.at[0], by.at[0], bc.at[0], f, f * X, f)
        v = apply(temp[...], zone_field(f))
        img[f] = v
        pack_faces(v, bface.at[1], bedge.at[1], f * X, f)
        return carry

    for c in order:
        wait_recv(first[c])
        if c == NC - 1:
            assemble(kext.at[0], src[K + 1], bx.at[0], by.at[0], bc.at[0], K + 1, (K + 1) * X, K + 1)
            kext[1] = zone_field(K + 1)
            k_all = kext[0]
            diag[...] = shift_value + 7.0 * k_all[1 : X + 1, :Y] + 0.5 * stencil(k_all, kext[1])
            lax.fori_loop(c * CHUNK, K + 1, image, 0)
            v = rhs[...] - img[K]
            img[K] = v
            pack_faces(v, bface.at[1], bedge.at[1], K * X, K)
        else:
            lax.fori_loop(c * CHUNK, (c + 1) * CHUNK, image, 0, unroll=2)
        start_halo(second[c])
    pack_lanes(lambda f: img[f], K + 1, 1)
    start_halo(second[NC])

    GR = gpart.shape[1]
    GW = Z // (GR // 8)
    assert K + 1 <= GW

    def gram_part(a, carry):
        va = img[a]
        rows = [tile_sum(img[b] * va) for b in range(K + 1)]
        rows.append(jnp.zeros((GR - K - 1, Z), f32))
        gpart[a] = jnp.concatenate(rows, axis=0)
        return carry

    lax.fori_loop(0, K + 1, gram_part, 0, unroll=2)
    lane_g = lax.broadcasted_iota(jnp.int32, (GR, Z), 1)
    gram = jnp.zeros((GR, Z), f32)
    for a in range(K + 1):
        gram = jnp.where(lane_g == a, jnp.sum(gpart[a], axis=1, keepdims=True), gram)
    def extend_all():
        for c in second:
            wait_recv(c)
        assemble_zones(1)

        def extend(f, carry):
            assemble(fields.at[f, 0], img[f], bx.at[1], by.at[1], bc.at[1], f, f * X, f)
            fields[f, 1] = zone_field(f)
            return carry

        lax.fori_loop(0, K + 1, extend, 0, unroll=4)

    part = gram[:8]
    for q in range(1, GR // 8):
        part = part + pltpu.roll(gram[8 * q : 8 * q + 8], q * GW, 1)
    part = all_reduce(part, TWO, (gred1, gred2), 2, extend_all)
    gram = [part] + [pltpu.roll(part, Z - q * GW, 1) for q in range(1, GR // 8)]
    gram = jnp.concatenate(gram, axis=0)

    lane_k = lax.broadcasted_iota(jnp.int32, (K, Z), 1)
    row_k = lax.broadcasted_iota(jnp.int32, (K, Z), 0)
    a_mat = jnp.where(lane_k < K, gram[:K], 0.0)
    for k in range(K):
        prow = a_mat[k : k + 1, :]
        pcol = a_mat[:, k : k + 1]
        inv_p = 1.0 / a_mat[k : k + 1, k : k + 1]
        prow_s = jnp.where(lax.broadcasted_iota(jnp.int32, (1, Z), 1) == k, 1.0, prow) * inv_p
        base = jnp.where(lane_k == k, 0.0, a_mat)
        a_mat = jnp.where(row_k == k, jnp.broadcast_to(prow_s, (K, Z)), base - pcol * prow_s)
    mat[...] = jnp.where(lane2 == row2, 1.0, 0.0)
    mat[0:K, :] = a_mat
    grow = jnp.where(lax.broadcasted_iota(jnp.int32, (1, Z), 1) < K, gram[K : K + 1, :], 0.0)
    ecoef[...] = jnp.broadcast_to(jnp.sum(a_mat * grow, axis=1, keepdims=True), (K, Z))

    def begin(p, carry):
        z, x = lax.div(p, X + 2), lax.rem(p, X + 2)
        v = fields[C0, z, x]
        for a in range(K):
            v = v - ecoef[a : a + 1, :] * fields[a, z, x]
        fields[C0, z, x] = v
        return carry

    lax.fori_loop(0, 2 * (X + 2), begin, 0)
    for c in first + second:
        wait_send(c)
    hcols[...] = jnp.zeros((32, Z), f32)
    scale[...] = jnp.where(row2 < K, 1.0, 0.0)

    def step(j, carry):
        par = lax.rem(j, 2)
        u = fields[C0 + j, 0]
        w = apply(u, fields[C0 + j, 1])
        wbuf[par, 0] = w
        pack_faces(w, wface.at[par], wedge.at[par], 0, 0)
        cs = step_copies(par)

        @pl.when(j < STEPS - 1)
        def _():
            start_halo(cs)

        rows = [tile_sum(fields[f, 0, 1 : X + 1, 0:Y, :] * w) for f in range(K + STEPS)]
        ui = u[1 : X + 1, :Y]
        rows.append(tile_sum(w * w))
        rows.append(tile_sum(ui * ui))
        rows.append(jnp.zeros((32 - K - STEPS - 2, Z), f32))
        sums = jnp.sum(jnp.concatenate(rows, axis=0), axis=1, keepdims=True)
        part = jnp.sum(jnp.where(lane2 == row2, sums, 0.0), axis=0, keepdims=True)
        def extend_w():
            @pl.when(j < STEPS - 1)
            def _():
                wait_recv(cs)
                slot = 2 + par
                assemble(temp, wbuf[par, 0], mx.at[par], my.at[par], mc.at[par], 0, 0, 0)
                fields[C0 + 1 + j, 0] = temp[...]
                assemble_zones(slot)
                fields[C0 + 1 + j, 1] = jnp.where(
                    lane3 == Z - 1, zext[0], jnp.where(lane3 == 0, zext[1], 0.0)
                )

            @pl.when(j == STEPS - 1)
            def _():
                fields[C0 + STEPS, 0, 1 : X + 1, 0:Y, :] = wbuf[par, 0]

        total = all_reduce(part, groups, (sred1.at[par], sred2.at[par]), par, extend_w)
        c = jnp.broadcast_to(jnp.sum(mat[...] * total, axis=1, keepdims=True), (32, Z))
        uu = c[K + STEPS + 1 : K + STEPS + 2, :]
        sc = jnp.where(row2 == C0 + j, 1.0 / uu, scale[...])
        scale[...] = sc
        hcols[...] = jnp.where(lane2 == j, c, hcols[...])
        inv_n = 1.0 / jnp.sqrt(uu)
        coef[...] = jnp.where(
            row2 < K + STEPS, c * sc * inv_n, jnp.where(row2 == 30, inv_n, total)
        )

        def update(p, carry):
            z, x = lax.div(p, X + 2), lax.rem(p, X + 2)
            v = coef[30:31, :] * fields[C0 + 1 + j, z, x]
            v2 = jnp.zeros_like(v)
            for a in range(0, K + STEPS, 2):
                v = v - coef[a : a + 1, :] * fields[a, z, x]
                v2 = v2 - coef[a + 1 : a + 2, :] * fields[a + 1, z, x]
            fields[C0 + 1 + j, z, x] = v + v2
            return carry

        lax.fori_loop(0, 2 * (X + 2), update, 0, unroll=4)

        @pl.when(j < STEPS - 1)
        def _():
            wait_send(cs)

        return carry

    lax.fori_loop(0, STEPS, step, 0)

    lane8 = lane2[:8]
    row8 = row2[:8]
    hc = hcols[...]
    inv_n2 = scale[C0 : C0 + STEPS, :]
    inv_col = jnp.sqrt(inv_n2)
    n_col = 1.0 / inv_col
    inv_row = jnp.sum(jnp.where(lane8 == row8, inv_col, 0.0), axis=0, keepdims=True)
    last_c = jnp.sum(jnp.where(lane2 == STEPS - 1, hc, 0.0), axis=1, keepdims=True)
    raw = jnp.broadcast_to(coef[31:32, :], (32, Z))
    raw_col = jnp.sum(jnp.where(lane2 == row2, raw, 0.0), axis=1, keepdims=True)
    terms = jnp.where(row2[:, :1] < K + STEPS, raw_col * last_c * scale[:, :1], 0.0)
    used = jnp.sum(terms, axis=0, keepdims=True)
    last_sq = (raw_col[K + STEPS : K + STEPS + 1] - used) * inv_n2[STEPS - 1 : STEPS, :1]
    last_n = jnp.sqrt(last_sq)
    upper = hc[C0 : C0 + STEPS] * inv_col * inv_row
    upper = jnp.where(lane8 < STEPS, upper, 0.0)
    upper = jnp.where(lane8 == row8 - 1, n_col, upper)
    lane1 = lane2[:1]
    bottom = jnp.where(lane1 == STEPS - 1, last_n, 0.0)
    hes = jnp.concatenate([upper, bottom], axis=0)
    hes_out[...] = hes[:, :STEPS]

    rows = [hes[i : i + 1] for i in range(STEPS + 1)]
    rows[0] = jnp.where(lane1 == STEPS, n_col[0:1], rows[0])
    for i in range(STEPS):
        top, low = rows[i][:, i : i + 1], rows[i + 1][:, i : i + 1]
        inv_r = 1.0 / jnp.sqrt(top * top + low * low)
        cs_, sn = top * inv_r, low * inv_r
        rows[i], rows[i + 1] = cs_ * rows[i] + sn * rows[i + 1], cs_ * rows[i + 1] - sn * rows[i]
    ysol = jnp.zeros((1, Z), f32)
    for i in range(STEPS - 1, -1, -1):
        known = jnp.sum(jnp.where(lane1 > i, rows[i] * ysol, 0.0), axis=1, keepdims=True)
        yi = (rows[i][:, STEPS : STEPS + 1] - known) / rows[i][:, i : i + 1]
        ysol = jnp.where(lane1 == i, yi, ysol)

    rcoef = ecoef[:, :1] - jnp.sum(hc[:K] * (ysol * inv_row), axis=1, keepdims=True)
    ycol = jnp.sum(jnp.where(lane8 == row8, ysol * inv_row, 0.0), axis=1, keepdims=True)
    hy8 = jnp.sum(upper * ysol, axis=1, keepdims=True) * inv_col[:, :1]
    hy9 = jnp.sum(bottom * ysol, axis=1, keepdims=True) / last_n
    out = guess[...]
    for a in range(K):
        out = out + rcoef[a : a + 1, :] * rec[a]
    res = fields[C0, 0, 1 : X + 1, 0:Y, :]
    for i in range(STEPS):
        ui = fields[C0 + i, 0, 1 : X + 1, 0:Y, :]
        out = out + ycol[i : i + 1, :] * ui
        res = res - hy8[i : i + 1, :] * ui
    res = res - hy9 * fields[C0 + STEPS, 0, 1 : X + 1, 0:Y, :]
    sol_out[...] = out
    res_out[...] = res


def deliver(sol, res, hes, sol_out, res_out, hes_out):
    sol_out[...] = sol[...]
    res_out[...] = res[...]
    hes_out[...] = hes[...]


def round_up(n, m):
    return (n + m - 1) // m * m


def solution(mesh):
    sizes = tuple(mesh.shape[a] for a in AXES)

    def body(right_side, start_guess, conductivity, recycled):
        K, X, Y, Z = recycled.shape
        NF = K + 2
        FR, ER, XR = round_up(NF * X, 8), round_up(NF, 8), round_up(X, 8)
        def count(group):
            n = 1
            for a in group:
                n *= mesh.shape[a]
            return n

        groups = ONE if count(AXES) <= 64 else TWO
        n_two, n_step = [count(g) for g in TWO], [count(g) for g in groups]
        biggest = max(n_two + n_step)
        nc = (NF + CHUNK - 1) // CHUNK
        GR = round_up(K + 1, 8)
        V = lambda *s: pltpu.VMEM(s, jnp.float32)
        vm = pl.BlockSpec(memory_space=pltpu.VMEM)
        shape = jax.ShapeDtypeStruct((X, Y, Z), jnp.float32)
        sol, res, hes = pl.pallas_call(
            functools.partial(kernel, sizes, groups),
            out_shape=(shape, shape, jax.ShapeDtypeStruct((STEPS + 1, STEPS), jnp.float32)),
            in_specs=[vm] * 4,
            out_specs=(vm, vm, vm),
            scratch_shapes=[
                V(NF, X, Y, Z), V(NF, X, Y, Z),
                V(2, 2, FR, Z), V(2, 2, 2, ER, Z),
                V(2, 2, 1, X, Y, Z), V(2, 2, 2, XR, Z), V(2, 2, 2, 2, 1, Z),
                V(2, 2, NF, Y, Z), V(2, 2, FR, Z), V(2, 2, 2, ER, Z),
                V(4, 2, 1, X, Y, Z), V(4, 2, 2, 1, Y, Z), V(4, 2, 2, XR, Z), V(4, 2, 2, 2, 1, Z),
                V(2, 2, 1, Y, Z), V(2, 2, XR, Z), V(2, 2, 2, 1, Z),
                V(2, 1, X, Y, Z), V(2, 2, XR, Z), V(2, 2, 2, 1, Z),
                V(K + STEPS + 1, 2, X + 2, Y + 8, Z), V(2, X + 2, Y + 8, Z), V(X, Y, Z),
                V(X + 2, Y + 8, Z), V(2, X + 2, Y + 8, Z),
                V(K + 1, GR, Z), V(n_two[0], 8, Z), V(n_two[1], 8, Z),
                V(2, n_step[0], 1, Z), V(2, n_step[-1], 1, Z),
                V(32, Z), V(32, Z), V(32, Z), V(32, Z), V(K, Z),
                pltpu.SemaphoreType.DMA((2 * nc + 4, 26)), pltpu.SemaphoreType.DMA((2 * nc + 4, 26)),
                pltpu.SemaphoreType.DMA((3, 2, biggest)), pltpu.SemaphoreType.DMA((3, 2, biggest)),
            ],
            compiler_params=pltpu.CompilerParams(collective_id=0, has_side_effects=True),
        )(right_side, start_guess, conductivity, recycled)
        return pl.pallas_call(
            deliver,
            out_shape=(shape, shape, jax.ShapeDtypeStruct(hes.shape, hes.dtype)),
            in_specs=[vm] * 3,
            out_specs=(vm,) * 3,
        )(sol, res, hes)

    return jax.shard_map(
        body,
        mesh=mesh,
        in_specs=(P(*AXES), P(*AXES), P(*AXES), P(None, *AXES)),
        out_specs=(P(*AXES), P(*AXES), P()),
        check_vma=False,
    )
```

profile of v0, /device:TPU:0, one launch (start us, length us, event | category | flops | bytes accessed | tf_op | source)
XLA Modules:
  0.0 83.4 jit_solution(3106026503953451667)
XLA Ops:
  0.6 80.0 %shard_map.67 = (f32[4,16,128]{2,1,0:T(8,128)}, f32[4,16,128]{2,1,0:T(8,128)}, f32[9,8]{1,0:T(8,128)}) custom-call(f32[4,16,128]{2,1,0:T(8,128)} %rhs.1, f32[4,16,128]{2,1,0:T(8,128)} %guess.1, f32[4,16,128]{2,1,0:T(8,128)} %cond.1, f32[16,4,16,128]{3,2,1,0:T(8,128)} %rec.1), custom_call_target="tpu_custom_call" | custom-call | tf_op jit(solution)/shard_map/pallas_call | solution.py:522
  80.7 1.4 %shard_map.68 = (f32[4,16,128]{2,1,0:T(8,128)}, f32[4,16,128]{2,1,0:T(8,128)}, f32[9,8]{1,0:T(8,128)}) custom-call(f32[4,16,128]{2,1,0:T(8,128)} %get-tuple-element.6.sol, f32[4,16,128]{2,1,0:T(8,128)} %get-tuple-element.7.res, f32[9,8]{1,0:T(8,128)} %get-tuple-element.8.hes), custom_call_target="tpu_custom_call" | custom-call | tf_op jit(solution)/shard_map/pallas_call | solution.py:545
  82.1 1.4 %copy.7 = f32[9,8]{0,1:T(8,128)} copy(f32[9,8]{1,0:T(8,128)} %get-tuple-element.11) | data formatting | bytes 576 | tf_op jit(solution)/shard_map/pallas_call | solution.py:545
where the time goes:
time: 83.7 us; the launch traced here: 83.4 us
  Pallas kernels  81.4 us (97%)
  local copies, waits for them, and re-layouts  1.36 us (2%)
    pallas_call x1, Pallas kernels, body(): pl.pallas_call(functools.partial(kernel, sizes, groups), out_shape=(shape...  80 us

commit v1 on v0

--- a/solution.py
+++ b/solution.py
@@ -14,12 +14,20 @@
 TWO = (("py", "pz"), ("px",))
 ONE = (("px", "py", "pz"),)
 CHUNK = 8
+GF = 4
 
 edge_weight = 0.25 ** (1.0 / 3.0)
 middle_weight = 2.0 * edge_weight
 shift_value = 0.4
 
 DIRS = [d for d in itertools.product((-1, 0, 1), repeat=3) if d != (0, 0, 0)]
+
+
+def sem_counts(sizes):
+    dirs = [d for d in DIRS if all(s == 0 or n > 1 for n, s in zip(sizes, d))]
+    flat = sum(d[2] == 0 for d in dirs)
+    tall = len(dirs) - flat
+    return flat, tall // 2 if sizes[2] == 2 else tall
 
 
 def kernel(
@@ -41,6 +49,7 @@
     K, X, Y, Z = rec.shape
     NF = K + 2
     C0 = K
+    NC = (NF + CHUNK - 1) // CHUNK
     f32 = jnp.float32
     lane3 = lax.broadcasted_iota(jnp.int32, (X + 2, Y + 8, Z), 2)
     lane2 = lax.broadcasted_iota(jnp.int32, (32, Z), 1)
@@ -58,7 +67,16 @@
     def possible(d):
         return all(s == 0 or nsz[a] > 1 for a, s in zip(AXES, d))
 
-    dirs = [(i, d) for i, d in enumerate(DIRS) if possible(d)]
+    flat = [d for d in DIRS if possible(d) and d[2] == 0]
+    tall = [d for d in DIRS if possible(d) and d[2] != 0]
+    dirs = flat + tall
+    NFLAT, NTALL = sem_counts(sizes)
+
+    def sem_index(chunk, d):
+        if d[2] == 0:
+            return chunk * NFLAT + flat.index(d)
+        twin = (d[0], d[1], 1) if nsz["pz"] == 2 else d
+        return NC * NFLAT + tall.index(twin) % NTALL
 
     def target(d):
         return tuple(me[a] + s for a, s in zip(AXES, d))
@@ -78,9 +96,9 @@
             r = lax.div(r, nsz[a])
         return tuple(co[a] for a in AXES)
 
-    def copies(sends, recvs, slot, zones):
+    def copies(sends, recvs, batch, chunk, zones):
         out = []
-        for i, (dx, dy, dz) in dirs:
+        for dx, dy, dz in dirs:
             if (dz != 0) not in zones:
                 continue
             main, face, edge = sends(dz)
@@ -97,7 +115,7 @@
             d = (dx, dy, dz)
             out.append((d, pltpu.make_async_remote_copy(
                 src_ref=s, dst_ref=t,
-                send_sem=hsend.at[slot, i], recv_sem=hrecv.at[slot, i],
+                send_sem=hsend.at[sem_index(chunk, d)], recv_sem=hrecv.at[batch, sem_index(chunk, d)],
                 device_id=target(d), device_id_type=MESH,
             )))
         return out
@@ -113,8 +131,6 @@
     def wait_send(cs):
         for d, c in cs:
             pl.when(exists(d))(c.wait_send)
-
-    NC = (NF + CHUNK - 1) // CHUNK
 
     def batch_copies(b, c):
         f0, f1 = c * CHUNK, min((c + 1) * CHUNK, NF)
@@ -134,7 +150,7 @@
             h = int(z > 0)
             return zm.at[b, h], zx.at[b, h], zy.at[b, h], zc.at[b, h]
 
-        return copies(sends, recvs, b * (NC + 1) + c, (c == NC,))
+        return copies(sends, recvs, b, c % NC, (c == NC,))
 
     def step_copies(par):
         def sends(dz):
@@ -146,7 +162,7 @@
             h = int(z > 0)
             return zm.at[2 + par, h], zx.at[2 + par, h], zy.at[2 + par, h], zc.at[2 + par, h]
 
-        return copies(sends, recvs, 2 * (NC + 1) + par, (False, True))
+        return copies(sends, recvs, par, 0, (False, True))
 
     def pack_faces(val, face, edge, row, erow):
         for h, y in ((0, 0), (1, Y - 1)):
@@ -211,29 +227,25 @@
             n, rank = group_info(group)
             buf = bufs[g]
             buf[rank] = total
-            cs = []
             for k in sorted(range(1, n), key=lambda k: -min(k, n - k)):
-                c = pltpu.make_async_remote_copy(
+                pltpu.make_async_remote_copy(
                     src_ref=buf.at[rank], dst_ref=buf.at[rank],
-                    send_sem=rsend.at[slot, g, k], recv_sem=rrecv.at[slot, g, k],
+                    send_sem=rsend.at[slot, g], recv_sem=rrecv.at[slot, g],
                     device_id=member(group, lax.rem(rank + k, n)), device_id_type=MESH,
-                )
-                c.start()
-                cs.append((k, c))
+                ).start()
             if g == len(groups) - 1:
                 between()
-            for k, c in cs:
-                pltpu.make_async_remote_copy(
-                    src_ref=buf.at[rank], dst_ref=buf.at[lax.rem(rank + n - k, n)],
-                    send_sem=rsend.at[slot, g, k], recv_sem=rrecv.at[slot, g, k],
-                    device_id=member(group, lax.rem(rank + k, n)), device_id_type=MESH,
-                ).wait_recv()
+            others = pltpu.make_async_remote_copy(
+                src_ref=buf.at[pl.ds(0, n - 1)], dst_ref=buf.at[pl.ds(0, n - 1)],
+                send_sem=rsend.at[slot, g], recv_sem=rrecv.at[slot, g],
+                device_id=member(group, lax.rem(rank + 1, n)), device_id_type=MESH,
+            )
+            others.wait_recv()
             parts = [buf[r] for r in range(n)]
             while len(parts) > 1:
                 parts = [sum(parts[r : r + 2][1:], parts[r]) for r in range(0, len(parts), 2)]
             total = parts[0]
-            for k, c in cs:
-                c.wait_send()
+            others.wait_send()
         return total
 
     def clear_all(refs):
@@ -302,12 +314,14 @@
             pack_faces(v, bface.at[1], bedge.at[1], K * X, K)
         else:
             lax.fori_loop(c * CHUNK, (c + 1) * CHUNK, image, 0, unroll=2)
+        wait_send(first[c])
         start_halo(second[c])
     pack_lanes(lambda f: img[f], K + 1, 1)
+    wait_send(first[NC])
     start_halo(second[NC])
 
     GR = gpart.shape[1]
-    GW = Z // (GR // 8)
+    GW = Z // (GR // GF)
     assert K + 1 <= GW
 
     def gram_part(a, carry):
@@ -334,11 +348,11 @@
 
         lax.fori_loop(0, K + 1, extend, 0, unroll=4)
 
-    part = gram[:8]
-    for q in range(1, GR // 8):
-        part = part + pltpu.roll(gram[8 * q : 8 * q + 8], q * GW, 1)
-    part = all_reduce(part, TWO, (gred1, gred2), 2, extend_all)
-    gram = [part] + [pltpu.roll(part, Z - q * GW, 1) for q in range(1, GR // 8)]
+    part = gram[:GF]
+    for q in range(1, GR // GF):
+        part = part + pltpu.roll(gram[GF * q : GF * q + GF], q * GW, 1)
+    part = all_reduce(part, groups, (gred1, gred2), 2, extend_all)
+    gram = [part] + [pltpu.roll(part, Z - q * GW, 1) for q in range(1, GR // GF)]
     gram = jnp.concatenate(gram, axis=0)
 
     lane_k = lax.broadcasted_iota(jnp.int32, (K, Z), 1)
@@ -365,7 +379,7 @@
         return carry
 
     lax.fori_loop(0, 2 * (X + 2), begin, 0)
-    for c in first + second:
+    for c in second:
         wait_send(c)
     hcols[...] = jnp.zeros((32, Z), f32)
     scale[...] = jnp.where(row2 < K, 1.0, 0.0)
@@ -456,7 +470,10 @@
     lane1 = lane2[:1]
     bottom = jnp.where(lane1 == STEPS - 1, last_n, 0.0)
     hes = jnp.concatenate([upper, bottom], axis=0)
-    hes_out[...] = hes[:, :STEPS]
+    lane_t, row_t = lane2[: STEPS + 1], row2[: STEPS + 1]
+    for col in range(STEPS):
+        picked = jnp.where(lane_t == row_t, hes[:, col : col + 1], 0.0)
+        hes_out[col : col + 1, :] = jnp.sum(picked, axis=0, keepdims=True)[:, : STEPS + 1]
 
     rows = [hes[i : i + 1] for i in range(STEPS + 1)]
     rows[0] = jnp.where(lane1 == STEPS, n_col[0:1], rows[0])
@@ -512,16 +529,16 @@
             return n
 
         groups = ONE if count(AXES) <= 64 else TWO
-        n_two, n_step = [count(g) for g in TWO], [count(g) for g in groups]
-        biggest = max(n_two + n_step)
-        nc = (NF + CHUNK - 1) // CHUNK
+        n_step = [count(g) for g in groups]
+        nflat, ntall = sem_counts(sizes)
+        nsem = (NF + CHUNK - 1) // CHUNK * nflat + ntall
         GR = round_up(K + 1, 8)
         V = lambda *s: pltpu.VMEM(s, jnp.float32)
         vm = pl.BlockSpec(memory_space=pltpu.VMEM)
         shape = jax.ShapeDtypeStruct((X, Y, Z), jnp.float32)
         sol, res, hes = pl.pallas_call(
             functools.partial(kernel, sizes, groups),
-            out_shape=(shape, shape, jax.ShapeDtypeStruct((STEPS + 1, STEPS), jnp.float32)),
+            out_shape=(shape, shape, jax.ShapeDtypeStruct((STEPS, STEPS + 1), jnp.float32)),
             in_specs=[vm] * 4,
             out_specs=(vm, vm, vm),
             scratch_shapes=[
@@ -534,20 +551,21 @@
                 V(2, 1, X, Y, Z), V(2, 2, XR, Z), V(2, 2, 2, 1, Z),
                 V(K + STEPS + 1, 2, X + 2, Y + 8, Z), V(2, X + 2, Y + 8, Z), V(X, Y, Z),
                 V(X + 2, Y + 8, Z), V(2, X + 2, Y + 8, Z),
-                V(K + 1, GR, Z), V(n_two[0], 8, Z), V(n_two[1], 8, Z),
+                V(K + 1, GR, Z), V(n_step[0], GF, Z), V(n_step[-1], GF, Z),
                 V(2, n_step[0], 1, Z), V(2, n_step[-1], 1, Z),
                 V(32, Z), V(32, Z), V(32, Z), V(32, Z), V(K, Z),
-                pltpu.SemaphoreType.DMA((2 * nc + 4, 26)), pltpu.SemaphoreType.DMA((2 * nc + 4, 26)),
-                pltpu.SemaphoreType.DMA((3, 2, biggest)), pltpu.SemaphoreType.DMA((3, 2, biggest)),
+                pltpu.SemaphoreType.DMA((nsem,)), pltpu.SemaphoreType.DMA((2, nsem)),
+                pltpu.SemaphoreType.DMA((3, len(groups))), pltpu.SemaphoreType.DMA((3, len(groups))),
             ],
             compiler_params=pltpu.CompilerParams(collective_id=0, has_side_effects=True),
         )(right_side, start_guess, conductivity, recycled)
-        return pl.pallas_call(
+        sol, res, hes = pl.pallas_call(
             deliver,
             out_shape=(shape, shape, jax.ShapeDtypeStruct(hes.shape, hes.dtype)),
             in_specs=[vm] * 3,
             out_specs=(vm,) * 3,
         )(sol, res, hes)
+        return sol, res, hes.T
 
     return jax.shard_map(
         body,

time: 83.7 us -> 73.2 us (0.87)
  Pallas kernels: 81.4 us -> 72.4 us
  local copies, waits for them, and re-layouts: 1.36 us -> 0 us
    pallas_call x1, Pallas kernels: 80 us -> 71 us  [body(): pl.pallas_call(functools.partial(kernel, sizes, groups), out_shape=(shape...]
    pallas_call x1 -> x0, local copies, waits for them, and re-layouts: 1.36 us -> none  [body(): pl.pallas_call(deliver, out_shape=(shape, shape, jax.ShapeDtypeStruct(hes...]
where the time goes in v1:
time: 73.2 us; the launch traced here: 73 us
  Pallas kernels  72.4 us (99%)
    pallas_call x1, Pallas kernels, body(): pl.pallas_call(functools.partial(kernel, sizes, groups), out_shape=(shape...  71 us

profile of v1, /device:TPU:0, one launch (start us, length us, event | category | flops | bytes accessed | tf_op | source)
XLA Modules:
  0.0 73.0 jit_solution(8721197436805672744)
XLA Ops:
  0.6 71.0 %shard_map.67 = (f32[4,16,128]{2,1,0:T(8,128)}, f32[4,16,128]{2,1,0:T(8,128)}, f32[8,9]{1,0:T(8,128)}) custom-call(f32[4,16,128]{2,1,0:T(8,128)} %rhs.1, f32[4,16,128]{2,1,0:T(8,128)} %guess.1, f32[4,16,128]{2,1,0:T(8,128)} %cond.1, f32[16,4,16,128]{3,2,1,0:T(8,128)} %rec.1), custom_call_target="tpu_custom_call" | custom-call | tf_op jit(solution)/shard_map/pallas_call | solution.py:539
  71.6 1.4 %shard_map.68 = (f32[4,16,128]{2,1,0:T(8,128)}, f32[4,16,128]{2,1,0:T(8,128)}, f32[8,9]{1,0:T(8,128)}) custom-call(f32[4,16,128]{2,1,0:T(8,128)} %get-tuple-element.9.sol, f32[4,16,128]{2,1,0:T(8,128)} %get-tuple-element.10.res, f32[8,9]{1,0:T(8,128)} %get-tuple-element.11.hes), custom_call_target="tpu_custom_call" | custom-call | tf_op jit(solution)/shard_map/pallas_call | solution.py:562

commit v2 on v1

v2 whole, which is shorter than its diff:
```python
import functools
import itertools

import jax
import jax.numpy as jnp
from jax import lax
from jax.experimental import pallas as pl
from jax.experimental.pallas import tpu as pltpu
from jax.sharding import PartitionSpec as P

STEPS = 8
MESH = pl.DeviceIdType.MESH
AXES = ("px", "py", "pz")
TWO = (("py", "pz"), ("px",))
ONE = (("px", "py", "pz"),)
CHUNK = 8
GF = 4
DEEP = 3
PAIR = 2
VROWS = 24

shift_value = 0.4
SHIFT = 2.8

DIRS = [d for d in itertools.product((-1, 0, 1), repeat=3) if d != (0, 0, 0)]


def sem_counts(sizes):
    dirs = [d for d in DIRS if all(s == 0 or n > 1 for n, s in zip(sizes, d))]
    flat = sum(d[2] == 0 for d in dirs)
    tall = len(dirs) - flat
    return flat, tall // 2 if sizes[2] == 2 else tall


def shell_cells(s):
    return [(i, j) for i in range(1, s + 1) for j in range(1, s + 1) if max(i, j) == s]


def square_cells(d):
    return [(i, j) for i in range(1, d + 1) for j in range(1, d + 1)]


def kernel(
    sizes, groups,
    rhs, guess, cond, rec,
    sol_out, res_out, hes_out,
    src, img, awf,
    aface, aedge, ax, ay, ac,
    bface1, bedge1, bx1, by1, bc1,
    bface2, bedge2, bx2, by2, bc2,
    bface3, bedge3, bx3, by3, bc3,
    pack0, pface0, pedge0, zm0, zx0, zy0, zc0,
    pack1, pface1, pedge1, zm1, zx1, zy1, zc1,
    wbuf, wface, wedge, mx, my, mc, zm2, zx2, zy2, zc2,
    fields, kext, dext, temp, zext, pe,
    gpart, npart, gred1, gred2, nred1, nred2, sred1, sred2,
    mat, na, gmat, n2mat, hcols, nsq, coefa, coefb, ecoef,
    hsend, hrecv, rsend, rrecv,
):
    nsz = dict(zip(AXES, sizes))
    me = {a: lax.axis_index(a) for a in AXES}
    K, X, Y, Z = rec.shape
    NF = K + 2
    C0 = K
    XE, YE = X + 2 * DEEP, Y + 8
    NC = (NF + CHUNK - 1) // CHUNK
    f32 = jnp.float32
    lane_p = lax.broadcasted_iota(jnp.int32, (YE, Z), 1)
    lane2 = lax.broadcasted_iota(jnp.int32, (32, Z), 1)
    row2 = lax.broadcasted_iota(jnp.int32, (32, Z), 0)
    row1 = row2[:, :1]
    lane1 = lane2[:1]

    def exists(d):
        ok = None
        for a, s in zip(AXES, d):
            if s == 0:
                continue
            here = (me[a] < nsz[a] - 1) if s > 0 else (me[a] > 0)
            ok = here if ok is None else jnp.logical_and(ok, here)
        return ok

    def possible(d):
        return all(s == 0 or nsz[a] > 1 for a, s in zip(AXES, d))

    flat = [d for d in DIRS if possible(d) and d[2] == 0]
    tall = [d for d in DIRS if possible(d) and d[2] != 0]
    dirs = flat + tall
    NFLAT, NTALL = sem_counts(sizes)

    def sem_index(chunk, d):
        if d[2] == 0:
            return NTALL + chunk * NFLAT + flat.index(d)
        twin = (d[0], d[1], 1) if nsz["pz"] == 2 else d
        return tall.index(twin) % NTALL

    def target(d):
        return tuple(me[a] + s for a, s in zip(AXES, d))

    def group_info(group):
        n = 1
        rank = 0
        for a in group:
            n *= nsz[a]
            rank = rank * nsz[a] + me[a]
        return n, rank

    def member(group, r):
        co = dict(me)
        for a in reversed(group):
            co[a] = lax.rem(r, nsz[a])
            r = lax.div(r, nsz[a])
        return tuple(co[a] for a in AXES)

    def copies(sends, recvs, batch, chunk, zones):
        out = []
        for dx, dy, dz in dirs:
            if (dz != 0) not in zones:
                continue
            main, xsl, face, edge = sends(dz)
            rm, rx, ry, rc = recvs(-dz)
            hx, hy = int(dx > 0), int(dy > 0)
            if dx == 0 and dy == 0:
                s, t = main, rm
            elif dy == 0:
                s, t = main.at[:, xsl[hx]], rx.at[1 - hx]
            elif dx == 0:
                s, t = face.at[hy], ry.at[1 - hy]
            else:
                s, t = edge.at[hx, hy], rc.at[1 - hx, 1 - hy]
            d = (dx, dy, dz)
            out.append((d, pltpu.make_async_remote_copy(
                src_ref=s, dst_ref=t,
                send_sem=hsend.at[sem_index(chunk, d)], recv_sem=hrecv.at[batch, sem_index(chunk, d)],
                device_id=target(d), device_id_type=MESH,
            )))
        return out

    def start_halo(cs):
        for d, c in cs:
            pl.when(exists(d))(c.start)

    def wait_recv(cs):
        for d, c in cs:
            pl.when(exists(tuple(-s for s in d)))(c.wait_recv)

    def wait_send(cs):
        for d, c in cs:
            pl.when(exists(d))(c.wait_send)

    def ends(d):
        return pl.ds(0, d), pl.ds(X - d, d)

    def batch_copies(b, c):
        f0, f1 = c * CHUNK, min((c + 1) * CHUNK, NF)
        fs, es = pl.ds(f0, f1 - f0), pl.ds(f0, CHUNK)
        depth = DEEP if b else 1
        wholes = (img, bface1, bedge1, bx1, by1, bc1) if b else (src, aface, aedge, ax, ay, ac)
        lanes = (
            (pack1, pface1, pedge1, zm1, zx1, zy1, zc1) if b
            else (pack0, pface0, pedge0, zm0, zx0, zy0, zc0)
        )
        rows = pl.ds(f0 * X, min(CHUNK * X, aface.shape[1] - f0 * X))

        def sends(dz):
            if dz == 0:
                main, face, edge = wholes[:3]
                return main.at[fs], ends(1), face.at[:, rows], edge.at[:, :, es]
            h = int(dz > 0)
            return lanes[0].at[h], ends(depth), lanes[1].at[h], lanes[2].at[h]

        def recvs(z):
            if z == 0:
                rx, ry, rc = wholes[3:]
                return None, rx.at[:, fs], ry.at[:, rows], rc.at[:, :, es]
            h = int(z > 0)
            return tuple(r.at[h] for r in lanes[3:])

        return copies(sends, recvs, b, c % NC, (c == NC,))

    def shell_copies(s):
        face, edge, rx, ry, rc = (
            (bface2, bedge2, bx2, by2, bc2) if s == 2 else (bface3, bedge3, bx3, by3, bc3)
        )
        planes = pl.ds(s - 1, 1), pl.ds(X - s, 1)
        return copies(
            lambda dz: (img, planes, face, edge), lambda z: (None, rx, ry, rc),
            0, NC + s - 2, (False,),
        )

    def pair_copies(par):
        def sends(dz):
            return wbuf.at[par], ends(PAIR), wface.at[par], wedge.at[par]

        def recvs(z):
            if z == 0:
                return None, mx.at[par], my.at[par], mc.at[par]
            h = int(z > 0)
            return zm2.at[par, h], zx2.at[par, h], zy2.at[par, h], zc2.at[par, h]

        return copies(sends, recvs, par, 0, (False, True))

    def pack_edges(row_of, face, edge, frow, erow, depths, cells):
        for n, i in enumerate(depths):
            for x in range(X):
                at = pl.ds(frow + n * X + x, 1)
                face[0, at, :] = row_of(x, i - 1)
                face[1, at, :] = row_of(x, Y - i)
        for n, (i, j) in enumerate(cells):
            for hx, hy in itertools.product((0, 1), repeat=2):
                edge[hx, hy, pl.ds(erow + n, 1), :] = row_of(
                    X - i if hx else i - 1, Y - j if hy else j - 1
                )

    def value_rows(val):
        return lambda x, y: val[x, y : y + 1, :]

    def ref_rows(ref, f):
        return lambda x, y: ref[f, x, y : y + 1, :]

    def place_edges(dst, ry, rc, frow, erow, depths, cells):
        for n, i in enumerate(depths):
            for x in range(X):
                at = pl.ds(frow + n * X + x, 1)
                dst[DEEP + x, Y + i - 1 : Y + i, :] = ry[1, at, :]
                dst[DEEP + x, YE - i : YE - i + 1, :] = ry[0, at, :]
        for n, (i, j) in enumerate(cells):
            for hx, hy in itertools.product((0, 1), repeat=2):
                x = DEEP + X + i - 1 if hx else DEEP - i
                y = Y + j - 1 if hy else YE - j
                dst[x, y : y + 1, :] = rc[hx, hy, pl.ds(erow + n, 1), :]

    def place_shell(dst, rx, ry, rc, f, s):
        cells = shell_cells(s)
        dst[DEEP - s, 0:Y, :] = rx[0, f, 0]
        dst[DEEP + X + s - 1, 0:Y, :] = rx[1, f, 0]
        place_edges(dst, ry, rc, f * X, f * len(cells), (s,), cells)

    def place_all(dst, main, rx, ry, rc, f, depth):
        cells = square_cells(depth)
        dst[DEEP : DEEP + X, 0:Y, :] = main[f]
        dst[DEEP - depth : DEEP, 0:Y, :] = rx[0, f]
        dst[DEEP + X : DEEP + X + depth, 0:Y, :] = rx[1, f]
        place_edges(
            dst, ry, rc, f * X * depth, f * len(cells), tuple(range(1, depth + 1)), cells
        )

    def zone_plane(f, x, depth):
        low = pltpu.roll(zext[0, x], lax.rem(2 * Z - depth - depth * f, Z), 1)
        high = pltpu.roll(zext[1, x], lax.rem(Z - depth * f, Z), 1)
        return jnp.where(lane_p >= Z - depth, low, jnp.where(lane_p < depth, high, 0.0))

    def pack_lanes(get, count, depth, pack, pface, pedge):
        lane = lax.broadcasted_iota(jnp.int32, (X, Y, Z), 2)
        low = jnp.zeros((X, Y, Z), f32)
        high = jnp.zeros((X, Y, Z), f32)
        for f in range(count):
            v = get(f)
            here = jnp.logical_and(lane >= depth * f, lane < depth * (f + 1))
            low = jnp.where(here, pltpu.roll(v, depth * f, 2) if f else v, low)
            high = jnp.where(here, pltpu.roll(v, (depth * (f + 1)) % Z, 2), high)
        for h, v in ((0, low), (1, high)):
            pack[h, 0] = v
            pack_edges(
                value_rows(v), pface.at[h], pedge.at[h], 0, 0,
                tuple(range(1, depth + 1)), square_cells(depth),
            )

    def sum_zy(e, b):
        left = pltpu.roll(jnp.where(lane_p == Z - 1, b, e), 1, 1)
        right = pltpu.roll(jnp.where(lane_p == 0, b, e), Z - 1, 1)
        t = (left + right) + (e + e)
        return (pltpu.roll(t, 1, 0) + pltpu.roll(t, YE - 1, 0)) + (t + t)

    def apply(get, zone, lo, hi, rows, use):
        sums = {}
        for x in range(lo - 1, hi + 1):
            e, b = get(zone, x), get(1 - zone, x)
            k, kb = kext[zone, x], kext[1 - zone, x]
            sums[x] = (e[:rows], k[:rows], sum_zy(e, b)[:rows], sum_zy(k * e, kb * b)[:rows])
            if x > lo:
                e0, k0, s0, t0 = sums[x - 1]
                near = (sums[x - 2][2] + sums[x][2]) + (s0 + s0)
                far = (sums[x - 2][3] + sums[x][3]) + (t0 + t0)
                use(x - 1, dext[zone, x - 1, :rows] * e0 - k0 * near - far, k0)

    def make_diag(shift):
        for z in range(2):
            sums = [sum_zy(kext[z, x], kext[1 - z, x]) for x in range(XE)]
            for x in range(1, XE - 1):
                total = (sums[x - 1] + sums[x + 1]) + (sums[x] + sums[x])
                dext[z, x] = (shift_value - shift) + 64.0 * kext[z, x] + total

    def tile_sum(v):
        v = jnp.sum(v.reshape(X * Y // 8, 8, Z), axis=0)
        return jnp.sum(v, axis=0, keepdims=True)

    def reduce_start(value, bufs, slot, g):
        group = groups[g]
        n, rank = group_info(group)
        buf = bufs[g]
        buf[rank] = value
        for k in sorted(range(1, n), key=lambda k: -min(k, n - k)):
            pltpu.make_async_remote_copy(
                src_ref=buf.at[rank], dst_ref=buf.at[rank],
                send_sem=rsend.at[slot, g], recv_sem=rrecv.at[slot, g],
                device_id=member(group, lax.rem(rank + k, n)), device_id_type=MESH,
            ).start()

    def reduce_end(bufs, slot, g):
        group = groups[g]
        n, rank = group_info(group)
        buf = bufs[g]
        others = pltpu.make_async_remote_copy(
            src_ref=buf.at[pl.ds(0, n - 1)], dst_ref=buf.at[pl.ds(0, n - 1)],
            send_sem=rsend.at[slot, g], recv_sem=rrecv.at[slot, g],
            device_id=member(group, lax.rem(rank + 1, n)), device_id_type=MESH,
        )
        others.wait_recv()
        parts = [buf[r] for r in range(n)]
        while len(parts) > 1:
            parts = [sum(parts[r : r + 2][1:], parts[r]) for r in range(0, len(parts), 2)]
        others.wait_send()
        return parts[0]

    def reduce_rest(bufs, slot):
        total = reduce_end(bufs, slot, 0)
        for g in range(1, len(groups)):
            reduce_start(total, bufs, slot, g)
            total = reduce_end(bufs, slot, g)
        return total

    def clear_all(refs):
        for ref in refs:
            def clear(i, carry, ref=ref):
                ref[i] = jnp.zeros(ref.shape[1:], f32)
                return carry

            lax.fori_loop(0, ref.shape[0], clear, 0)

    clear_all((ax, ay, ac, bx1, by1, bc1, bx2, by2, bc2, bx3, by3, bc3))
    clear_all((zm0, zx0, zy0, zc0, zm1, zx1, zy1, zc1, mx, my, mc, zm2, zx2, zy2, zc2))
    barrier = pltpu.get_barrier_semaphore()
    count = jnp.int32(0)
    for group in ONE:
        n, rank = group_info(group)
        for k in range(1, n):
            pl.semaphore_signal(
                barrier, inc=1, device_id=member(group, lax.rem(rank + k, n)), device_id_type=MESH
            )
        count = count + (n - 1)

    clear_all((wface, wedge, aface, aedge, bface1, bedge1, bface2, bedge2, bface3, bedge3))
    clear_all((pface0, pedge0, pface1, pedge1))

    near_cells = shell_cells(1)

    def load_field(f, carry):
        v = rec[f]
        src[f] = v
        pack_edges(value_rows(v), aface, aedge, f * X, f, (1,), near_cells)
        return carry

    lax.fori_loop(0, K, load_field, 0)
    for f, v in ((K, guess[...]), (K + 1, 0.125 * cond[...])):
        src[f] = v
        pack_edges(value_rows(v), aface, aedge, f * X, f, (1,), near_cells)
    pack_lanes(lambda f: src[f], NF, 1, pack0, pface0, pedge0)
    pl.semaphore_wait(barrier, count)

    first = [batch_copies(0, c) for c in range(NC + 1)]
    second = [batch_copies(1, c) for c in range(NC + 1)]
    order = [NC - 1] + list(range(NC - 1))
    for c in [NC] + order:
        start_halo(first[c])
    clear_all((fields, kext, dext, zext, pe))
    temp[...] = jnp.zeros(temp.shape, f32)
    img[NF - 1] = src[NF - 1]
    pack_edges(
        ref_rows(src, NF - 1), bface1, bedge1, (NF - 1) * X, NF - 1, (1,), near_cells
    )
    wait_recv(first[NC])
    for h in range(2):
        place_all(zext.at[h], zm0.at[h], zx0.at[h], zy0.at[h], zc0.at[h], 0, 1)

    def image(f, carry):
        dst = temp.at[0]
        dst[DEEP : DEEP + X, 0:Y, :] = src[f]
        place_shell(dst, ax, ay, ac, f, 1)
        for x in range(DEEP - 1, DEEP + X + 1):
            temp[1, x] = zone_plane(f, x, 1)

        def use(x, v, k):
            img[f, x - DEEP] = v

        apply(lambda z, x: temp[z, x], 0, DEEP, DEEP + X, Y, use)
        pack_edges(ref_rows(img, f), bface1, bedge1, f * X, f, (1,), near_cells)
        return carry

    for c in order:
        wait_recv(first[c])
        if c == NC - 1:
            kext[0, DEEP : DEEP + X, 0:Y, :] = src[K + 1]
            place_shell(kext.at[0], ax, ay, ac, K + 1, 1)
            for x in range(DEEP - 1, DEEP + X + 1):
                kext[1, x] = zone_plane(K + 1, x, 1)
            make_diag(0.0)
            lax.fori_loop(c * CHUNK, K + 1, image, 0)
            img[K] = rhs[...] - img[K]
            pack_edges(ref_rows(img, K), bface1, bedge1, K * X, K, (1,), near_cells)
        else:
            lax.fori_loop(c * CHUNK, (c + 1) * CHUNK, image, 0)
        wait_send(first[c])
        start_halo(second[c])
    pack_lanes(lambda f: img[f], NF, DEEP, pack1, pface1, pedge1)
    wait_send(first[NC])
    start_halo(second[NC])

    GR = gpart.shape[1]
    GW = Z // (GR // GF)
    assert K + 1 <= GW and DEEP * NF <= Z

    def gram_part(a, carry):
        va = img[a]
        rows = [tile_sum(img[b] * va) for b in range(K + 1)]
        rows.append(jnp.zeros((GR - K - 1, Z), f32))
        gpart[a] = jnp.concatenate(rows, axis=0)
        return carry

    lax.fori_loop(0, K + 1, gram_part, 0, unroll=2)
    lane_g = lax.broadcasted_iota(jnp.int32, (GR, Z), 1)
    gram = jnp.zeros((GR, Z), f32)
    for a in range(K + 1):
        gram = jnp.where(lane_g == a, jnp.sum(gpart[a], axis=1, keepdims=True), gram)
    part = gram[:GF]
    for q in range(1, GR // GF):
        part = part + pltpu.roll(gram[GF * q : GF * q + GF], q * GW, 1)
    reduce_start(part, (gred1, gred2), 2, 0)

    shells = {2: shell_copies(2), 3: shell_copies(3)}
    for s, face, edge in ((2, bface2, bedge2), (3, bface3, bedge3)):
        cells = shell_cells(s)

        def pack_shell(f, carry, s=s, face=face, edge=edge, cells=cells):
            pack_edges(ref_rows(img, f), face, edge, f * X, f * len(cells), (s,), cells)
            return carry

        lax.fori_loop(0, NF, pack_shell, 0)
        start_halo(shells[s])

    for c in second:
        wait_recv(c)
    for h in range(2):
        place_all(zext.at[h], zm1.at[h], zx1.at[h], zy1.at[h], zc1.at[h], 0, DEEP)

    def inner(f, carry):
        fields[f, 0, DEEP : DEEP + X, 0:Y, :] = img[f]
        place_shell(fields.at[f, 0], bx1, by1, bc1, f, 1)
        for x in range(XE):
            fields[f, 1, x] = zone_plane(f, x, DEEP)
        return carry

    lax.fori_loop(0, K + 1, inner, 0)
    for x in range(XE):
        kext[1, x] = zone_plane(K + 1, x, DEEP)
    make_diag(SHIFT)

    def second_image(f, carry):
        def use(x, v, k):
            awf[f, x - DEEP] = v

        apply(lambda z, x: fields[f, z, x], 0, DEEP, DEEP + X, Y, use)
        return carry

    lax.fori_loop(0, K, second_image, 0)

    def cross_part(a, carry):
        va, vb = img[a], awf[a]
        rows = []
        for b in range(K):
            vw = awf[b]
            rows.append((tile_sum(vw * va), tile_sum(vw * vb)))
        npart[a] = jnp.concatenate([r[0] for r in rows] + [r[1] for r in rows], axis=0)
        return carry

    lax.fori_loop(0, K, cross_part, 0)
    cross = jnp.zeros((2 * K, Z), f32)
    lane_n = lax.broadcasted_iota(jnp.int32, (2 * K, Z), 1)
    for a in range(K):
        cross = jnp.where(lane_n == a, jnp.sum(npart[a], axis=1, keepdims=True), cross)
    NW = Z // (2 * K // GF)
    assert K <= NW
    part = cross[:GF]
    for q in range(1, 2 * K // GF):
        part = part + pltpu.roll(cross[GF * q : GF * q + GF], q * NW, 1)
    reduce_start(part, (nred1, nred2), 3, 0)

    def outer(s, rx, ry, rc):
        wait_recv(shells[s])

        def place(f, carry):
            place_shell(fields.at[f, 0], rx, ry, rc, f, s)
            return carry

        lax.fori_loop(0, K + 1, place, 0)
        place_shell(kext.at[0], rx, ry, rc, K + 1, s)
        make_diag(SHIFT)

    outer(2, bx2, by2, bc2)

    part = reduce_rest((gred1, gred2), 2)
    gram = [part] + [pltpu.roll(part, Z - q * GW, 1) for q in range(1, GR // GF)]
    gram = jnp.concatenate(gram, axis=0)

    lane_k = lax.broadcasted_iota(jnp.int32, (K, Z), 1)
    row_k = lax.broadcasted_iota(jnp.int32, (K, Z), 0)
    a_mat = jnp.where(lane_k < K, gram[:K], 0.0)
    gmat[...] = a_mat
    for k in range(K):
        prow = a_mat[k : k + 1, :]
        pcol = a_mat[:, k : k + 1]
        inv_p = 1.0 / a_mat[k : k + 1, k : k + 1]
        prow_s = jnp.where(lane1 == k, 1.0, prow) * inv_p
        base = jnp.where(lane_k == k, 0.0, a_mat)
        a_mat = jnp.where(row_k == k, jnp.broadcast_to(prow_s, (K, Z)), base - pcol * prow_s)
    mat[...] = jnp.where(
        row2 < VROWS, jnp.where(lane2 == row2, 1.0, 0.0),
        jnp.where(lane2 == row2 + VROWS, 1.0, 0.0),
    )
    mat[0:K, :] = a_mat
    grow = jnp.where(lane1 < K, gram[K : K + 1, :], 0.0)
    ecoef[...] = jnp.broadcast_to(jnp.sum(a_mat * grow, axis=1, keepdims=True), (K, Z))

    def begin(p, carry):
        z, x = lax.rem(p, 2), DEEP - PAIR + lax.div(p, 2)
        v = fields[C0, z, x]
        for a in range(K):
            v = v - ecoef[a : a + 1, :] * fields[a, z, x]
        fields[C0, z, x] = v
        return carry

    lax.fori_loop(0, 2 * (X + 2 * PAIR), begin, 0)
    for c in second:
        wait_send(c)
    hcols[...] = jnp.zeros((32, Z), f32)
    nsq[...] = jnp.ones((32, Z), f32)

    def col_sum(v):
        return jnp.sum(v, axis=0, keepdims=True)

    def lane_sum(v):
        return jnp.sum(v, axis=1, keepdims=True)

    def finish_cross():
        part = reduce_rest((nred1, nred2), 3)
        both = [part] + [pltpu.roll(part, Z - q * NW, 1) for q in range(1, 2 * K // GF)]
        both = jnp.where(lane_n < K, jnp.concatenate(both, axis=0), 0.0)
        na[...] = both[:K]
        n2mat[...] = both[K:]

    def record(j, c1, c2, t1, q1, q2, uu, ww):
        old = hcols[...]
        q_lane = col_sum(jnp.where((lane2 == row2 - K) & (lane2 < j), c1, 0.0))
        c3 = c2 - q1 * c1 - lane_sum(old * q_lane)
        c3 = jnp.where(row1 < VROWS, c3, 0.0)
        e_lane = col_sum(jnp.where((lane2 == row2) & (row2 < K), c3, 0.0))
        ge = lane_sum(gmat[...] * e_lane)
        now = jnp.where(row1 == K + j + 1, 1.0, c1)
        then = jnp.where(row1 == K + j + 1, q2, jnp.where(row1 == K + j + 2, 1.0, c3))
        hcols[...] = jnp.where(lane2 == j, now, jnp.where(lane2 == j + 1, then, old))
        nv = na[...]
        nv = jnp.where(lane_k == K + j, t1[:K], jnp.where(lane_k == K + j + 1, ge, nv))
        na[...] = nv
        new = jnp.where(row2 == K + j, uu, jnp.where(row2 == K + j + 1, ww, nsq[...]))
        nsq[...] = new
        fresh = jnp.logical_and(lane2 == row2, (row2 == K + j) | (row2 == K + j + 1))
        mat[...] = jnp.where(fresh, 1.0 / new, mat[...])

    pending = []
    last_sq = None
    for j in range(0, STEPS, 2):
        last = j == STEPS - 2
        par = (j // 2) % 2
        u = fields.at[C0 + j]
        p1r, p2r = pe.at[0], pe.at[1]

        for zone in range(2):
            def use(x, v, k, zone=zone):
                p1r[zone, x] = jnp.where(k > 0.0, v, 0.0)

            apply(lambda z, x: u[z, x], zone, DEEP - 1, DEEP + X + 1, YE, use)

        def use(x, v, k):
            wbuf[par, 1, x - DEEP] = v

        apply(lambda z, x: p1r[z, x], 0, DEEP, DEEP + X, Y, use)
        p1 = p1r[0, DEEP : DEEP + X, 0:Y, :]
        p2 = wbuf[par, 1]
        wbuf[par, 0] = p1
        if not last:
            for n, v in ((0, p1), (1, p2)):
                cells = square_cells(PAIR)
                pack_edges(
                    value_rows(v), wface.at[par], wedge.at[par], n * X * PAIR,
                    n * len(cells), tuple(range(1, PAIR + 1)), cells,
                )

        rows1, rows2 = [], []
        for f in range(K + j + 1):
            v = fields[f, 0, DEEP : DEEP + X, 0:Y, :]
            rows1.append(tile_sum(v * p1))
            rows2.append(tile_sum(v * p2))
        fill = [jnp.zeros((VROWS - K - j - 1, Z), f32)] if K + j + 1 < VROWS else []
        rows = rows1 + fill + rows2 + fill
        uin = u[0, DEEP : DEEP + X, 0:Y, :]
        rows += [tile_sum(p1 * p1), tile_sum(p1 * p2), tile_sum(p2 * p2), tile_sum(uin * uin)]
        rows.append(jnp.zeros((4, Z), f32))
        if last:
            rows += [tile_sum(awf[a] * p2) for a in range(K)]
        R = 2 * VROWS + 8 + (K if last else 0)
        lane_r = lax.broadcasted_iota(jnp.int32, (R, Z), 1)
        row_r = lax.broadcasted_iota(jnp.int32, (R, Z), 0)
        sums = lane_sum(jnp.concatenate(rows, axis=0))
        part = col_sum(jnp.where(lane_r == row_r, sums, 0.0))
        bufs = (sred1.at[par], sred2.at[par])
        reduce_start(part, bufs, par, 0)
        if not last:
            cs = pair_copies(par)
            if j == 0:
                for s in shells:
                    wait_send(shells[s])
            start_halo(cs)
        if j == 0:
            outer(3, bx3, by3, bc3)
            finish_cross()
        for p in pending:
            record(*p)
        if not last:
            wait_recv(cs)
            for n in range(2):
                place_all(pe.at[n, 0], wbuf.at[par], mx.at[par], my.at[par], mc.at[par], n, PAIR)
                for h in range(2):
                    place_all(
                        zext.at[h], zm2.at[par, h], zx2.at[par, h], zy2.at[par, h],
                        zc2.at[par, h], n, PAIR,
                    )
                for x in range(DEEP - PAIR, DEEP + X + PAIR):
                    pe[n, 1, x] = jnp.where(
                        lane_p >= Z - PAIR, zext[0, x],
                        jnp.where(lane_p < PAIR, zext[1, x], 0.0),
                    )
        else:
            pe[1, 0, DEEP : DEEP + X, 0:Y, :] = p2
        total = reduce_rest(bufs, par)

        m = mat[...]
        c1 = lane_sum(m * total)
        p11, p12, p22, uu = (c1[VROWS + n : VROWS + n + 1] for n in range(4))
        inv_uu = 1.0 / uu
        c1 = jnp.where(row1 == K + j, c1 * inv_uu, jnp.where(row1 < VROWS, c1, 0.0))
        t1 = lane_sum(jnp.where((lane2 == row2) & (row2 < VROWS), total, 0.0))
        t2 = lane_sum(jnp.where((lane2 == row2 + VROWS) & (row2 < K), total, 0.0))
        nv = jnp.where(lane_k == K + j, t1[:K], na[...])
        low = col_sum(nv * c1[:K])
        diff = pltpu.roll(total, Z - VROWS, 1) - low
        c2 = lane_sum(m * diff)
        c2 = jnp.where(row1 == K + j, c2 * inv_uu, jnp.where(row1 < VROWS, c2, 0.0))
        ww = p11 - col_sum(t1 * c1)
        q1 = c1[K + j : K + j + 1]
        a2e = col_sum(t2 * c1)
        q2 = (p12 - col_sum(t1 * c2) - a2e) / ww - q1
        s = q1 + q2
        cc = c2 - s * c1
        coefa[...] = jnp.broadcast_to(c1, (32, Z))
        coefb[...] = jnp.broadcast_to(jnp.where(row1 == VROWS, s, cc), (32, Z))
        pending = [(j, c1, c2, t1, q1, q2, uu, ww)]
        if last:
            a3 = lane_sum(jnp.where(lane2 == row2 + 2 * VROWS + 8, total, 0.0))[:K]
            e1 = c1[:K]
            e_lane = col_sum(jnp.where(lane_k == row_k, e1, 0.0))
            n2e = lane_sum(n2mat[...] * e_lane)
            d_col = lane_sum(jnp.where((lane2 == row2) & (row2 < VROWS), diff, 0.0))
            last_sq = (
                p22 - s * p12 + s * a2e - col_sum(e1 * (2.0 * a3 - n2e)) - col_sum(cc * d_col)
            )

        p_lo, p_n = (DEEP - 1, X + 2) if last else (0, XE)

        def combine(p, carry, j=j, p_lo=p_lo):
            z, x = lax.rem(p, 2), p_lo + lax.div(p, 2)
            t = jnp.zeros((YE, Z), f32)
            g = jnp.zeros((YE, Z), f32)
            for a in range(K):
                w = fields[a, z, x]
                t = t + coefa[a : a + 1, :] * w
                g = g + coefb[a : a + 1, :] * w
            temp[z, x] = t
            v1 = pe[0, z, x]
            g = pe[1, z, x] - coefb[VROWS : VROWS + 1, :] * v1 - g
            v1 = v1 - t
            for a in range(K, K + j + 1):
                w = fields[a, z, x]
                v1 = v1 - coefa[a : a + 1, :] * w
                g = g - coefb[a : a + 1, :] * w
            fields[C0 + j + 1, z, x] = v1
            fields[C0 + j + 2, z, x] = g
            return carry

        lax.fori_loop(0, 2 * p_n, combine, 0)
        w2 = fields.at[C0 + j + 2]
        if last:
            def use(x, v, k):
                w2[0, x, 0:Y, :] = w2[0, x, 0:Y, :] - v

            apply(lambda z, x: temp[z, x], 0, DEEP, DEEP + X, Y, use)
        else:
            for zone in range(2):
                def use(x, v, k, zone=zone):
                    w2[zone, x] = w2[zone, x] - jnp.where(k > 0.0, v, 0.0)

                apply(
                    lambda z, x: temp[z, x], zone, DEEP - PAIR, DEEP + X + PAIR, YE, use
                )
            wait_send(cs)

    for p in pending:
        record(*p)

    lane8 = lane2[:8]
    row8 = row2[:8]
    hc = hcols[...]
    n2_col = nsq[C0 : C0 + STEPS, :]
    n_col = jnp.sqrt(n2_col)
    inv_col = 1.0 / n_col
    inv_row = col_sum(jnp.where(lane8 == row8, inv_col, 0.0))
    last_n = jnp.sqrt(last_sq)
    upper = hc[C0 : C0 + STEPS] * n_col * inv_row
    upper = jnp.where(lane8 < STEPS, upper, 0.0)
    upper = jnp.where(lane8 == row8, upper + SHIFT, upper)
    bottom = jnp.where(lane1 == STEPS - 1, last_n * inv_row, 0.0)
    hes = jnp.concatenate([upper, bottom], axis=0)
    lane_t, row_t = lane2[: STEPS + 1], row2[: STEPS + 1]
    for col in range(STEPS):
        picked = jnp.where(lane_t == row_t, hes[:, col : col + 1], 0.0)
        hes_out[col : col + 1, :] = jnp.sum(picked, axis=0, keepdims=True)[:, : STEPS + 1]

    rows = [hes[i : i + 1] for i in range(STEPS + 1)]
    rows[0] = jnp.where(lane1 == STEPS, n_col[0:1], rows[0])
    for i in range(STEPS):
        top, low = rows[i][:, i : i + 1], rows[i + 1][:, i : i + 1]
        inv_r = 1.0 / jnp.sqrt(top * top + low * low)
        cs_, sn = top * inv_r, low * inv_r
        rows[i], rows[i + 1] = cs_ * rows[i] + sn * rows[i + 1], cs_ * rows[i + 1] - sn * rows[i]
    ysol = jnp.zeros((1, Z), f32)
    for i in range(STEPS - 1, -1, -1):
        known = jnp.sum(jnp.where(lane1 > i, rows[i] * ysol, 0.0), axis=1, keepdims=True)
        yi = (rows[i][:, STEPS : STEPS + 1] - known) / rows[i][:, i : i + 1]
        ysol = jnp.where(lane1 == i, yi, ysol)

    rcoef = ecoef[:, :1] - jnp.sum(hc[:K] * (ysol * inv_row), axis=1, keepdims=True)
    ycol = jnp.sum(jnp.where(lane8 == row8, ysol * inv_row, 0.0), axis=1, keepdims=True)
    hy8 = jnp.sum(upper * ysol, axis=1, keepdims=True) * inv_col[:, :1]
    hy9 = jnp.sum(bottom * ysol, axis=1, keepdims=True) / last_n
    out = guess[...]
    for a in range(K):
        out = out + rcoef[a : a + 1, :] * rec[a]
    res = fields[C0, 0, DEEP : DEEP + X, 0:Y, :]
    for i in range(STEPS):
        ui = fields[C0 + i, 0, DEEP : DEEP + X, 0:Y, :]
        out = out + ycol[i : i + 1, :] * ui
        res = res - hy8[i : i + 1, :] * ui
    res = res - hy9 * fields[C0 + STEPS, 0, DEEP : DEEP + X, 0:Y, :]
    sol_out[...] = out
    res_out[...] = res


def deliver(sol, res, hes, sol_out, res_out, hes_out):
    sol_out[...] = sol[...]
    res_out[...] = res[...]
    hes_out[...] = hes[...]


def round_up(n, m):
    return (n + m - 1) // m * m


def solution(mesh):
    sizes = tuple(mesh.shape[a] for a in AXES)

    def body(right_side, start_guess, conductivity, recycled):
        K, X, Y, Z = recycled.shape
        NF = K + 2
        FR, ER = round_up(NF * X, 8), round_up(NF, 8)
        assert X >= DEEP and Y % 8 == 0 and K + STEPS <= VROWS

        def count(group):
            n = 1
            for a in group:
                n *= mesh.shape[a]
            return n

        groups = ONE if count(AXES) <= 64 else TWO
        n_step = [count(g) for g in groups]
        nflat, ntall = sem_counts(sizes)
        chunks = (NF + CHUNK - 1) // CHUNK
        nsem = ntall + (chunks + 2) * nflat
        GR = round_up(K + 1, 8)
        XE, YE = X + 2 * DEEP, Y + 8
        V = lambda *s: pltpu.VMEM(s, jnp.float32)
        vm = pl.BlockSpec(memory_space=pltpu.VMEM)
        shape = jax.ShapeDtypeStruct((X, Y, Z), jnp.float32)

        def halo(s):
            cells = 2 * s - 1
            return [
                V(2, FR, Z), V(2, 2, ER * cells, Z),
                V(2, NF, 1, Y, Z), V(2, FR, Z), V(2, 2, ER * cells, Z),
            ]

        def lanes(d):
            rows, cells = round_up(X * d, 8), d * d
            return [
                V(2, 1, X, Y, Z), V(2, 2, rows, Z), V(2, 2, 2, cells, Z),
                V(2, 1, X, Y, Z), V(2, 2, 1, d, Y, Z), V(2, 2, rows, Z), V(2, 2, 2, cells, Z),
            ]

        prow, pcell = round_up(2 * X * PAIR, 8), 2 * PAIR * PAIR
        sol, res, hes = pl.pallas_call(
            functools.partial(kernel, sizes, groups),
            out_shape=(shape, shape, jax.ShapeDtypeStruct((STEPS, STEPS + 1), jnp.float32)),
            in_specs=[vm] * 4,
            out_specs=(vm, vm, vm),
            scratch_shapes=[
                V(NF, X, Y, Z), V(NF, X, Y, Z), V(K, X, Y, Z),
                *halo(1), *halo(1), *halo(2), *halo(3), *lanes(1), *lanes(DEEP),
                V(2, 2, X, Y, Z), V(2, 2, prow, Z), V(2, 2, 2, pcell, Z),
                V(2, 2, 2, PAIR, Y, Z), V(2, 2, prow, Z), V(2, 2, 2, pcell, Z),
                V(2, 2, 2, X, Y, Z), V(2, 2, 2, 2, PAIR, Y, Z),
                V(2, 2, 2, prow, Z), V(2, 2, 2, 2, pcell, Z),
                V(K + STEPS + 1, 2, XE, YE, Z), V(2, XE, YE, Z), V(2, XE, YE, Z),
                V(2, XE, YE, Z), V(2, XE, YE, Z), V(2, 2, XE, YE, Z),
                V(K + 1, GR, Z), V(K, 2 * K, Z),
                V(n_step[0], GF, Z), V(n_step[-1], GF, Z), V(n_step[0], GF, Z), V(n_step[-1], GF, Z),
                V(2, n_step[0], 1, Z), V(2, n_step[-1], 1, Z),
                V(32, Z), V(K, Z), V(K, Z), V(K, Z), V(32, Z), V(32, Z), V(32, Z), V(32, Z), V(K, Z),
                pltpu.SemaphoreType.DMA((nsem,)), pltpu.SemaphoreType.DMA((2, nsem)),
                pltpu.SemaphoreType.DMA((4, len(groups))), pltpu.SemaphoreType.DMA((4, len(groups))),
            ],
            compiler_params=pltpu.CompilerParams(collective_id=0, has_side_effects=True),
        )(right_side, start_guess, conductivity, recycled)
        sol, res, hes = pl.pallas_call(
            deliver,
            out_shape=(shape, shape, jax.ShapeDtypeStruct(hes.shape, hes.dtype)),
            in_specs=[vm] * 3,
            out_specs=(vm,) * 3,
        )(sol, res, hes)
        return sol, res, hes.T

    return jax.shard_map(
        body,
        mesh=mesh,
        in_specs=(P(*AXES), P(*AXES), P(*AXES), P(None, *AXES)),
        out_specs=(P(*AXES), P(*AXES), P()),
        check_vma=False,
    )
```

time: 73.2 us -> 66.3 us (0.906)
  Pallas kernels: 72.4 us -> 65.4 us
    pallas_call x1, Pallas kernels: 71 us -> 64 us  [body(): pl.pallas_call(functools.partial(kernel, sizes, groups), out_shape=(shape...]
where the time goes in v2:
time: 66.3 us; the launch traced here: 66.1 us
  Pallas kernels  65.4 us (99%)
    pallas_call x1, Pallas kernels, body(): pl.pallas_call(functools.partial(kernel, sizes, groups), out_shape=(shape...  64 us
    pallas_call x1, Pallas kernels, body(): pl.pallas_call(deliver, out_shape=(shape, shape, jax.ShapeDtypeStruct(hes...  1.41 us

profile of v2, /device:TPU:0, one launch (start us, length us, event | category | flops | bytes accessed | tf_op | source)
XLA Modules:
  0.0 66.1 jit_solution(1361505128875524063)
XLA Ops:
  0.6 64.0 %shard_map.67 = (f32[4,16,128]{2,1,0:T(8,128)}, f32[4,16,128]{2,1,0:T(8,128)}, f32[8,9]{1,0:T(8,128)}) custom-call(f32[4,16,128]{2,1,0:T(8,128)} %rhs.1, f32[4,16,128]{2,1,0:T(8,128)} %guess.1, f32[4,16,128]{2,1,0:T(8,128)} %cond.1, f32[16,4,16,128]{3,2,1,0:T(8,128)} %rec.1), custom_call_target="tpu_custom_call" | custom-call | tf_op jit(solution)/shard_map/pallas_call | solution.py:828
  64.7 1.4 %shard_map.68 = (f32[4,16,128]{2,1,0:T(8,128)}, f32[4,16,128]{2,1,0:T(8,128)}, f32[8,9]{1,0:T(8,128)}) custom-call(f32[4,16,128]{2,1,0:T(8,128)} %get-tuple-element.9.sol, f32[4,16,128]{2,1,0:T(8,128)} %get-tuple-element.10.res, f32[8,9]{1,0:T(8,128)} %get-tuple-element.11.hes), custom_call_target="tpu_custom_call" | custom-call | tf_op jit(solution)/shard_map/pallas_call | solution.py:851

commit v3 on v2

--- a/solution.py
+++ b/solution.py
@@ -42,9 +42,9 @@
 
 def kernel(
     sizes, groups,
-    rhs, guess, cond, rec,
+    rhs_hbm, guess_hbm, cond_hbm, rec_hbm,
     sol_out, res_out, hes_out,
-    src, img, awf,
+    rhs, cond, src, img, awf,
     aface, aedge, ax, ay, ac,
     bface1, bedge1, bx1, by1, bc1,
     bface2, bedge2, bx2, by2, bc2,
@@ -52,14 +52,14 @@
     pack0, pface0, pedge0, zm0, zx0, zy0, zc0,
     pack1, pface1, pedge1, zm1, zx1, zy1, zc1,
     wbuf, wface, wedge, mx, my, mc, zm2, zx2, zy2, zc2,
-    fields, kext, dext, temp, zext, pe,
-    gpart, npart, gred1, gred2, nred1, nred2, sred1, sred2,
+    fields, kext, dext, temp, zext, zw, pe,
+    gred1, gred2, nred1, nred2, sred1, sred2,
     mat, na, gmat, n2mat, hcols, nsq, coefa, coefb, ecoef,
-    hsend, hrecv, rsend, rrecv,
+    hsend, hrecv, rsend, rrecv, isem,
 ):
     nsz = dict(zip(AXES, sizes))
     me = {a: lax.axis_index(a) for a in AXES}
-    K, X, Y, Z = rec.shape
+    K, X, Y, Z = rec_hbm.shape
     NF = K + 2
     C0 = K
     XE, YE = X + 2 * DEEP, Y + 8
@@ -71,31 +71,39 @@
     row1 = row2[:, :1]
     lane1 = lane2[:1]
 
+    pair = nsz["pz"] == 2
+
     def exists(d):
         ok = None
         for a, s in zip(AXES, d):
-            if s == 0:
+            if s == 0 or (pair and a == "pz"):
                 continue
             here = (me[a] < nsz[a] - 1) if s > 0 else (me[a] > 0)
             ok = here if ok is None else jnp.logical_and(ok, here)
-        return ok
+        return True if ok is None else ok
+
+    def when(ok, f):
+        if ok is True:
+            f()
+        else:
+            pl.when(ok)(f)
 
     def possible(d):
-        return all(s == 0 or nsz[a] > 1 for a, s in zip(AXES, d))
+        return all(s == 0 or nsz[a] > 1 for a, s in zip(AXES, d)) and not (pair and d[2] < 0)
 
     flat = [d for d in DIRS if possible(d) and d[2] == 0]
     tall = [d for d in DIRS if possible(d) and d[2] != 0]
     dirs = flat + tall
-    NFLAT, NTALL = sem_counts(sizes)
+    NFLAT, NTALL = len(flat), len(tall)
 
     def sem_index(chunk, d):
         if d[2] == 0:
             return NTALL + chunk * NFLAT + flat.index(d)
-        twin = (d[0], d[1], 1) if nsz["pz"] == 2 else d
-        return tall.index(twin) % NTALL
+        return tall.index(d)
 
     def target(d):
-        return tuple(me[a] + s for a, s in zip(AXES, d))
+        x, y, z = (me[a] + s for a, s in zip(AXES, d))
+        return x, y, 1 - me["pz"] if pair and d[2] else z
 
     def group_info(group):
         n = 1
@@ -105,20 +113,14 @@
             rank = rank * nsz[a] + me[a]
         return n, rank
 
-    def member(group, r):
-        co = dict(me)
-        for a in reversed(group):
-            co[a] = lax.rem(r, nsz[a])
-            r = lax.div(r, nsz[a])
-        return tuple(co[a] for a in AXES)
-
     def copies(sends, recvs, batch, chunk, zones):
         out = []
         for dx, dy, dz in dirs:
             if (dz != 0) not in zones:
                 continue
             main, xsl, face, edge = sends(dz)
-            rm, rx, ry, rc = recvs(-dz)
+            side = None if dz == 0 else me["pz"] if pair else int(dz < 0)
+            rm, rx, ry, rc = recvs(side)
             hx, hy = int(dx > 0), int(dy > 0)
             if dx == 0 and dy == 0:
                 s, t = main, rm
@@ -131,22 +133,22 @@
             d = (dx, dy, dz)
             out.append((d, pltpu.make_async_remote_copy(
                 src_ref=s, dst_ref=t,
-                send_sem=hsend.at[sem_index(chunk, d)], recv_sem=hrecv.at[batch, sem_index(chunk, d)],
+                send_sem=hsend.at[sem_index(chunk, d)], recv_sem=hrecv.at[batch * (NTALL + NC * NFLAT) + sem_index(chunk, d)],
                 device_id=target(d), device_id_type=MESH,
             )))
         return out
 
     def start_halo(cs):
         for d, c in cs:
-            pl.when(exists(d))(c.start)
+            when(exists(d), c.start)
 
     def wait_recv(cs):
         for d, c in cs:
-            pl.when(exists(tuple(-s for s in d)))(c.wait_recv)
+            when(exists(tuple(-s for s in d)), c.wait_recv)
 
     def wait_send(cs):
         for d, c in cs:
-            pl.when(exists(d))(c.wait_send)
+            when(exists(d), c.wait_send)
 
     def ends(d):
         return pl.ds(0, d), pl.ds(X - d, d)
@@ -166,14 +168,12 @@
             if dz == 0:
                 main, face, edge = wholes[:3]
                 return main.at[fs], ends(1), face.at[:, rows], edge.at[:, :, es]
-            h = int(dz > 0)
-            return lanes[0].at[h], ends(depth), lanes[1].at[h], lanes[2].at[h]
-
-        def recvs(z):
-            if z == 0:
+            return lanes[0], ends(depth), lanes[1], lanes[2]
+
+        def recvs(h):
+            if h is None:
                 rx, ry, rc = wholes[3:]
                 return None, rx.at[:, fs], ry.at[:, rows], rc.at[:, :, es]
-            h = int(z > 0)
             return tuple(r.at[h] for r in lanes[3:])
 
         return copies(sends, recvs, b, c % NC, (c == NC,))
@@ -184,18 +184,17 @@
         )
         planes = pl.ds(s - 1, 1), pl.ds(X - s, 1)
         return copies(
-            lambda dz: (img, planes, face, edge), lambda z: (None, rx, ry, rc),
-            0, NC + s - 2, (False,),
+            lambda dz: (img, planes, face, edge), lambda h: (None, rx, ry, rc),
+            1, NC + s - 2, (False,),
         )
 
     def pair_copies(par):
         def sends(dz):
             return wbuf.at[par], ends(PAIR), wface.at[par], wedge.at[par]
 
-        def recvs(z):
-            if z == 0:
+        def recvs(h):
+            if h is None:
                 return None, mx.at[par], my.at[par], mc.at[par]
-            h = int(z > 0)
             return zm2.at[par, h], zx2.at[par, h], zy2.at[par, h], zc2.at[par, h]
 
         return copies(sends, recvs, par, 0, (False, True))
@@ -245,26 +244,31 @@
             dst, ry, rc, f * X * depth, f * len(cells), tuple(range(1, depth + 1)), cells
         )
 
+    def slots(depth):
+        return 2 * depth, lax.rem(lane_p, 2 * depth) < depth
+
     def zone_plane(f, x, depth):
-        low = pltpu.roll(zext[0, x], lax.rem(2 * Z - depth - depth * f, Z), 1)
-        high = pltpu.roll(zext[1, x], lax.rem(Z - depth * f, Z), 1)
-        return jnp.where(lane_p >= Z - depth, low, jnp.where(lane_p < depth, high, 0.0))
+        return pltpu.roll(zw[x], Z - depth - 2 * depth * f, 1)
+
+    def fill_zone(depth, zm, zx, zy, zc):
+        for h in range(2):
+            place_all(zext.at[h], zm.at[h], zx.at[h], zy.at[h], zc.at[h], 0, depth)
+        low = slots(depth)[1]
+        for x in range(DEEP - depth, DEEP + X + depth):
+            zw[x] = jnp.where(low, zext[0, x], zext[1, x])
 
     def pack_lanes(get, count, depth, pack, pface, pedge):
         lane = lax.broadcasted_iota(jnp.int32, (X, Y, Z), 2)
-        low = jnp.zeros((X, Y, Z), f32)
-        high = jnp.zeros((X, Y, Z), f32)
+        width = 2 * depth
+        v = jnp.zeros((X, Y, Z), f32)
         for f in range(count):
-            v = get(f)
-            here = jnp.logical_and(lane >= depth * f, lane < depth * (f + 1))
-            low = jnp.where(here, pltpu.roll(v, depth * f, 2) if f else v, low)
-            high = jnp.where(here, pltpu.roll(v, (depth * (f + 1)) % Z, 2), high)
-        for h, v in ((0, low), (1, high)):
-            pack[h, 0] = v
-            pack_edges(
-                value_rows(v), pface.at[h], pedge.at[h], 0, 0,
-                tuple(range(1, depth + 1)), square_cells(depth),
-            )
+            here = jnp.logical_and(lane >= width * f, lane < width * (f + 1))
+            v = jnp.where(here, pltpu.roll(get(f), width * f + depth, 2), v)
+        pack[0] = v
+        pack_edges(
+            value_rows(v), pface, pedge, 0, 0,
+            tuple(range(1, depth + 1)), square_cells(depth),
+        )
 
     def sum_zy(e, b):
         left = pltpu.roll(jnp.where(lane_p == Z - 1, b, e), 1, 1)
@@ -272,17 +276,25 @@
         t = (left + right) + (e + e)
         return (pltpu.roll(t, 1, 0) + pltpu.roll(t, YE - 1, 0)) + (t + t)
 
-    def apply(get, zone, lo, hi, rows, use):
-        sums = {}
+    def apply(get, zones, lo, hi, rows, use):
+        planes = {}
         for x in range(lo - 1, hi + 1):
-            e, b = get(zone, x), get(1 - zone, x)
-            k, kb = kext[zone, x], kext[1 - zone, x]
-            sums[x] = (e[:rows], k[:rows], sum_zy(e, b)[:rows], sum_zy(k * e, kb * b)[:rows])
+            now = []
+            for z in range(2):
+                e = get(z, x)
+                now += [e, kext[z, x] * e]
+            planes[x] = now
             if x > lo:
-                e0, k0, s0, t0 = sums[x - 1]
-                near = (sums[x - 2][2] + sums[x][2]) + (s0 + s0)
-                far = (sums[x - 2][3] + sums[x][3]) + (t0 + t0)
-                use(x - 1, dext[zone, x - 1, :rows] * e0 - k0 * near - far, k0)
+                sums = [
+                    (a + c) + (b + b) for a, b, c in zip(planes[x - 2], planes[x - 1], now)
+                ]
+                for z in zones:
+                    o = 1 - z
+                    k0 = kext[z, x - 1, :rows]
+                    near = sum_zy(sums[2 * z], sums[2 * o])[:rows]
+                    far = sum_zy(sums[2 * z + 1], sums[2 * o + 1])[:rows]
+                    e0 = planes[x - 1][2 * z][:rows]
+                    use(z, x - 1, dext[z, x - 1, :rows] * e0 - k0 * near - far, k0)
 
     def make_diag(shift):
         for z in range(2):
@@ -291,20 +303,70 @@
                 total = (sums[x - 1] + sums[x + 1]) + (sums[x] + sums[x])
                 dext[z, x] = (shift_value - shift) + 64.0 * kext[z, x] + total
 
-    def tile_sum(v):
-        v = jnp.sum(v.reshape(X * Y // 8, 8, Z), axis=0)
+    lane8 = lane2[:8]
+    row8 = row2[:8]
+
+    def fold(v):
+        return jnp.sum(v.reshape(X * Y // 8, 8, Z), axis=0)
+
+    def row_sums(parts):
+        parts = parts + [None] * (-len(parts) % 8)
+        for d in (1, 2, 4):
+            here = lax.rem(lax.div(row8, d), 2) == 0
+            merged = []
+            for a, b in zip(parts[::2], parts[1::2]):
+                if a is None:
+                    merged.append(None)
+                    continue
+                b = 0.0 if b is None else b
+                merged.append(jnp.where(here, a, b) + pltpu.roll(jnp.where(here, b, a), d, 0))
+            parts = merged
+        return jnp.concatenate(
+            [jnp.zeros((8, Z), f32) if p is None else p for p in parts], axis=0
+        )
+
+    def lane_sum(v):
+        return jnp.sum(v, axis=1, keepdims=True)
+
+    def col_sum(v):
         return jnp.sum(v, axis=0, keepdims=True)
+
+    def symmetric(n, rows, dots):
+        lane = lax.broadcasted_iota(jnp.int32, (rows, Z), 1)
+        row = lax.broadcasted_iota(jnp.int32, (rows, Z), 0)
+        out = jnp.zeros((rows, Z), f32)
+        for a in range(n):
+            col = lane_sum(row_sums(dots(a)))
+            if col.shape[0] < rows:
+                col = jnp.concatenate([col, jnp.zeros((rows - col.shape[0], 1), f32)], axis=0)
+            across = col_sum(jnp.where((lane == row) & (row < a), col, 0.0))
+            out = jnp.where(lane == a, col, jnp.where(row == a, across, out))
+        return out
+
+    spots = {}
+    for axis in AXES:
+        for o in range(nsz[axis]):
+            at = me[axis] + o
+            spots[axis, o] = jnp.where(at >= nsz[axis], at - nsz[axis], at) if o else at
+
+    def peers(group):
+        ways = list(itertools.product(*(range(nsz[a]) for a in group)))[1:]
+        far = lambda w: -sum(min(o, nsz[a] - o) for a, o in zip(group, w))
+        return [
+            tuple(spots[a, w[group.index(a)]] if a in group else me[a] for a in AXES)
+            for w in sorted(ways, key=far)
+        ]
 
     def reduce_start(value, bufs, slot, g):
         group = groups[g]
-        n, rank = group_info(group)
+        rank = group_info(group)[1]
         buf = bufs[g]
         buf[rank] = value
-        for k in sorted(range(1, n), key=lambda k: -min(k, n - k)):
+        for peer in peers(group):
             pltpu.make_async_remote_copy(
                 src_ref=buf.at[rank], dst_ref=buf.at[rank],
                 send_sem=rsend.at[slot, g], recv_sem=rrecv.at[slot, g],
-                device_id=member(group, lax.rem(rank + k, n)), device_id_type=MESH,
+                device_id=peer, device_id_type=MESH,
             ).start()
 
     def reduce_end(bufs, slot, g):
@@ -314,7 +376,7 @@
         others = pltpu.make_async_remote_copy(
             src_ref=buf.at[pl.ds(0, n - 1)], dst_ref=buf.at[pl.ds(0, n - 1)],
             send_sem=rsend.at[slot, g], recv_sem=rrecv.at[slot, g],
-            device_id=member(group, lax.rem(rank + 1, n)), device_id_type=MESH,
+            device_id=peers(group)[0], device_id_type=MESH,
         )
         others.wait_recv()
         parts = [buf[r] for r in range(n)]
@@ -338,33 +400,38 @@
 
             lax.fori_loop(0, ref.shape[0], clear, 0)
 
+    loads = [
+        pltpu.make_async_copy(a, b, isem.at[n])
+        for n, (a, b) in enumerate(
+            ((cond_hbm, cond), (guess_hbm, src.at[K]), (rec_hbm, src.at[pl.ds(0, K)]), (rhs_hbm, rhs))
+        )
+    ]
+    for c in loads:
+        c.start()
     clear_all((ax, ay, ac, bx1, by1, bc1, bx2, by2, bc2, bx3, by3, bc3))
     clear_all((zm0, zx0, zy0, zc0, zm1, zx1, zy1, zc1, mx, my, mc, zm2, zx2, zy2, zc2))
     barrier = pltpu.get_barrier_semaphore()
     count = jnp.int32(0)
     for group in ONE:
-        n, rank = group_info(group)
-        for k in range(1, n):
-            pl.semaphore_signal(
-                barrier, inc=1, device_id=member(group, lax.rem(rank + k, n)), device_id_type=MESH
-            )
-        count = count + (n - 1)
+        everyone = peers(group)
+        for peer in everyone:
+            pl.semaphore_signal(barrier, inc=1, device_id=peer, device_id_type=MESH)
+        count = count + len(everyone)
 
     clear_all((wface, wedge, aface, aedge, bface1, bedge1, bface2, bedge2, bface3, bedge3))
     clear_all((pface0, pedge0, pface1, pedge1))
 
     near_cells = shell_cells(1)
 
+    for c in loads:
+        c.wait()
+    src[K + 1] = 0.125 * cond[...]
+
     def load_field(f, carry):
-        v = rec[f]
-        src[f] = v
-        pack_edges(value_rows(v), aface, aedge, f * X, f, (1,), near_cells)
+        pack_edges(ref_rows(src, f), aface, aedge, f * X, f, (1,), near_cells)
         return carry
 
-    lax.fori_loop(0, K, load_field, 0)
-    for f, v in ((K, guess[...]), (K + 1, 0.125 * cond[...])):
-        src[f] = v
-        pack_edges(value_rows(v), aface, aedge, f * X, f, (1,), near_cells)
+    lax.fori_loop(0, NF, load_field, 0, unroll=2)
     pack_lanes(lambda f: src[f], NF, 1, pack0, pface0, pedge0)
     pl.semaphore_wait(barrier, count)
 
@@ -373,15 +440,14 @@
     order = [NC - 1] + list(range(NC - 1))
     for c in [NC] + order:
         start_halo(first[c])
-    clear_all((fields, kext, dext, zext, pe))
+    clear_all((fields, kext, dext, zext, zw, pe))
     temp[...] = jnp.zeros(temp.shape, f32)
     img[NF - 1] = src[NF - 1]
     pack_edges(
         ref_rows(src, NF - 1), bface1, bedge1, (NF - 1) * X, NF - 1, (1,), near_cells
     )
     wait_recv(first[NC])
-    for h in range(2):
-        place_all(zext.at[h], zm0.at[h], zx0.at[h], zy0.at[h], zc0.at[h], 0, 1)
+    fill_zone(1, zm0, zx0, zy0, zc0)
 
     def image(f, carry):
         dst = temp.at[0]
@@ -390,10 +456,10 @@
         for x in range(DEEP - 1, DEEP + X + 1):
             temp[1, x] = zone_plane(f, x, 1)
 
-        def use(x, v, k):
+        def use(z, x, v, k):
             img[f, x - DEEP] = v
 
-        apply(lambda z, x: temp[z, x], 0, DEEP, DEEP + X, Y, use)
+        apply(lambda z, x: temp[z, x], (0,), DEEP, DEEP + X, Y, use)
         pack_edges(ref_rows(img, f), bface1, bedge1, f * X, f, (1,), near_cells)
         return carry
 
@@ -403,35 +469,29 @@
             kext[0, DEEP : DEEP + X, 0:Y, :] = src[K + 1]
             place_shell(kext.at[0], ax, ay, ac, K + 1, 1)
             for x in range(DEEP - 1, DEEP + X + 1):
-                kext[1, x] = zone_plane(K + 1, x, 1)
+                v = zone_plane(K + 1, x, 1)
+                kext[1, x] = jnp.where((lane_p < 1) | (lane_p >= Z - 1), v, 0.0)
             make_diag(0.0)
             lax.fori_loop(c * CHUNK, K + 1, image, 0)
             img[K] = rhs[...] - img[K]
             pack_edges(ref_rows(img, K), bface1, bedge1, K * X, K, (1,), near_cells)
         else:
-            lax.fori_loop(c * CHUNK, (c + 1) * CHUNK, image, 0)
+            lax.fori_loop(c * CHUNK, (c + 1) * CHUNK, image, 0, unroll=2)
         wait_send(first[c])
         start_halo(second[c])
     pack_lanes(lambda f: img[f], NF, DEEP, pack1, pface1, pedge1)
     wait_send(first[NC])
     start_halo(second[NC])
 
-    GR = gpart.shape[1]
+    GR = (K + 8) // 8 * 8
     GW = Z // (GR // GF)
-    assert K + 1 <= GW and DEEP * NF <= Z
-
-    def gram_part(a, carry):
+    assert K + 1 <= GW and 2 * DEEP * NF <= Z
+
+    def gram_dots(a):
         va = img[a]
-        rows = [tile_sum(img[b] * va) for b in range(K + 1)]
-        rows.append(jnp.zeros((GR - K - 1, Z), f32))
-        gpart[a] = jnp.concatenate(rows, axis=0)
-        return carry
-
-    lax.fori_loop(0, K + 1, gram_part, 0, unroll=2)
-    lane_g = lax.broadcasted_iota(jnp.int32, (GR, Z), 1)
-    gram = jnp.zeros((GR, Z), f32)
-    for a in range(K + 1):
-        gram = jnp.where(lane_g == a, jnp.sum(gpart[a], axis=1, keepdims=True), gram)
+        return [fold(img[b] * va) for b in range(a + 1)]
+
+    gram = symmetric(K + 1, GR, gram_dots)
     part = gram[:GF]
     for q in range(1, GR // GF):
         part = part + pltpu.roll(gram[GF * q : GF * q + GF], q * GW, 1)
@@ -445,13 +505,12 @@
             pack_edges(ref_rows(img, f), face, edge, f * X, f * len(cells), (s,), cells)
             return carry
 
-        lax.fori_loop(0, NF, pack_shell, 0)
+        lax.fori_loop(0, NF, pack_shell, 0, unroll=2)
         start_halo(shells[s])
 
     for c in second:
         wait_recv(c)
-    for h in range(2):
-        place_all(zext.at[h], zm1.at[h], zx1.at[h], zy1.at[h], zc1.at[h], 0, DEEP)
+    fill_zone(DEEP, zm1, zx1, zy1, zc1)
 
     def inner(f, carry):
         fields[f, 0, DEEP : DEEP + X, 0:Y, :] = img[f]
@@ -460,34 +519,31 @@
             fields[f, 1, x] = zone_plane(f, x, DEEP)
         return carry
 
-    lax.fori_loop(0, K + 1, inner, 0)
+    lax.fori_loop(0, K + 1, inner, 0, unroll=4)
     for x in range(XE):
-        kext[1, x] = zone_plane(K + 1, x, DEEP)
+        v = zone_plane(K + 1, x, DEEP)
+        kext[1, x] = jnp.where((lane_p < DEEP) | (lane_p >= Z - DEEP), v, 0.0)
     make_diag(SHIFT)
 
     def second_image(f, carry):
-        def use(x, v, k):
+        def use(z, x, v, k):
             awf[f, x - DEEP] = v
 
-        apply(lambda z, x: fields[f, z, x], 0, DEEP, DEEP + X, Y, use)
+        apply(lambda z, x: fields[f, z, x], (0,), DEEP, DEEP + X, Y, use)
         return carry
 
-    lax.fori_loop(0, K, second_image, 0)
-
-    def cross_part(a, carry):
-        va, vb = img[a], awf[a]
-        rows = []
-        for b in range(K):
-            vw = awf[b]
-            rows.append((tile_sum(vw * va), tile_sum(vw * vb)))
-        npart[a] = jnp.concatenate([r[0] for r in rows] + [r[1] for r in rows], axis=0)
-        return carry
-
-    lax.fori_loop(0, K, cross_part, 0)
-    cross = jnp.zeros((2 * K, Z), f32)
+    lax.fori_loop(0, K, second_image, 0, unroll=2)
+
+    def cross_dots(a):
+        va = awf[a]
+        return [fold(img[b] * va) for b in range(a + 1)]
+
+    def square_dots(a):
+        va = awf[a]
+        return [fold(awf[b] * va) for b in range(a + 1)]
+
+    cross = jnp.concatenate([symmetric(K, K, cross_dots), symmetric(K, K, square_dots)], axis=0)
     lane_n = lax.broadcasted_iota(jnp.int32, (2 * K, Z), 1)
-    for a in range(K):
-        cross = jnp.where(lane_n == a, jnp.sum(npart[a], axis=1, keepdims=True), cross)
     NW = Z // (2 * K // GF)
     assert K <= NW
     part = cross[:GF]
@@ -502,7 +558,7 @@
             place_shell(fields.at[f, 0], rx, ry, rc, f, s)
             return carry
 
-        lax.fori_loop(0, K + 1, place, 0)
+        lax.fori_loop(0, K + 1, place, 0, unroll=2)
         place_shell(kext.at[0], rx, ry, rc, K + 1, s)
         make_diag(SHIFT)
 
@@ -539,17 +595,11 @@
         fields[C0, z, x] = v
         return carry
 
-    lax.fori_loop(0, 2 * (X + 2 * PAIR), begin, 0)
+    lax.fori_loop(0, 2 * (X + 2 * PAIR), begin, 0, unroll=4)
     for c in second:
         wait_send(c)
     hcols[...] = jnp.zeros((32, Z), f32)
     nsq[...] = jnp.ones((32, Z), f32)
-
-    def col_sum(v):
-        return jnp.sum(v, axis=0, keepdims=True)
-
-    def lane_sum(v):
-        return jnp.sum(v, axis=1, keepdims=True)
 
     def finish_cross():
         part = reduce_rest((nred1, nred2), 3)
@@ -584,16 +634,15 @@
         u = fields.at[C0 + j]
         p1r, p2r = pe.at[0], pe.at[1]
 
-        for zone in range(2):
-            def use(x, v, k, zone=zone):
-                p1r[zone, x] = jnp.where(k > 0.0, v, 0.0)
-
-            apply(lambda z, x: u[z, x], zone, DEEP - 1, DEEP + X + 1, YE, use)
-
-        def use(x, v, k):
+        def use(z, x, v, k):
+            p1r[z, x] = jnp.where(k > 0.0, v, 0.0)
+
+        apply(lambda z, x: u[z, x], (0, 1), DEEP - 1, DEEP + X + 1, YE, use)
+
+        def use(z, x, v, k):
             wbuf[par, 1, x - DEEP] = v
 
-        apply(lambda z, x: p1r[z, x], 0, DEEP, DEEP + X, Y, use)
+        apply(lambda z, x: p1r[z, x], (0,), DEEP, DEEP + X, Y, use)
         p1 = p1r[0, DEEP : DEEP + X, 0:Y, :]
         p2 = wbuf[par, 1]
         wbuf[par, 0] = p1
@@ -608,19 +657,18 @@
         rows1, rows2 = [], []
         for f in range(K + j + 1):
             v = fields[f, 0, DEEP : DEEP + X, 0:Y, :]
-            rows1.append(tile_sum(v * p1))
-            rows2.append(tile_sum(v * p2))
-        fill = [jnp.zeros((VROWS - K - j - 1, Z), f32)] if K + j + 1 < VROWS else []
-        rows = rows1 + fill + rows2 + fill
+            rows1.append(fold(v * p1))
+            rows2.append(fold(v * p2))
+        gap = [None] * (VROWS - K - j - 1)
         uin = u[0, DEEP : DEEP + X, 0:Y, :]
-        rows += [tile_sum(p1 * p1), tile_sum(p1 * p2), tile_sum(p2 * p2), tile_sum(uin * uin)]
-        rows.append(jnp.zeros((4, Z), f32))
+        rows = rows1 + gap + rows2 + gap
+        rows += [fold(p1 * p1), fold(p1 * p2), fold(p2 * p2), fold(uin * uin)] + [None] * 4
         if last:
-            rows += [tile_sum(awf[a] * p2) for a in range(K)]
+            rows += [fold(awf[a] * p2) for a in range(K)]
         R = 2 * VROWS + 8 + (K if last else 0)
         lane_r = lax.broadcasted_iota(jnp.int32, (R, Z), 1)
         row_r = lax.broadcasted_iota(jnp.int32, (R, Z), 0)
-        sums = lane_sum(jnp.concatenate(rows, axis=0))
+        sums = lane_sum(row_sums(rows))
         part = col_sum(jnp.where(lane_r == row_r, sums, 0.0))
         bufs = (sred1.at[par], sred2.at[par])
         reduce_start(part, bufs, par, 0)
@@ -706,28 +754,23 @@
             fields[C0 + j + 2, z, x] = g
             return carry
 
-        lax.fori_loop(0, 2 * p_n, combine, 0)
+        lax.fori_loop(0, 2 * p_n, combine, 0, unroll=2)
         w2 = fields.at[C0 + j + 2]
         if last:
-            def use(x, v, k):
+            def use(z, x, v, k):
                 w2[0, x, 0:Y, :] = w2[0, x, 0:Y, :] - v
 
-            apply(lambda z, x: temp[z, x], 0, DEEP, DEEP + X, Y, use)
+            apply(lambda z, x: temp[z, x], (0,), DEEP, DEEP + X, Y, use)
         else:
-            for zone in range(2):
-                def use(x, v, k, zone=zone):
-                    w2[zone, x] = w2[zone, x] - jnp.where(k > 0.0, v, 0.0)
-
-                apply(
-                    lambda z, x: temp[z, x], zone, DEEP - PAIR, DEEP + X + PAIR, YE, use
-                )
+            def use(z, x, v, k):
+                w2[z, x] = w2[z, x] - jnp.where(k > 0.0, v, 0.0)
+
+            apply(lambda z, x: temp[z, x], (0, 1), DEEP - PAIR, DEEP + X + PAIR, YE, use)
             wait_send(cs)
 
     for p in pending:
         record(*p)
 
-    lane8 = lane2[:8]
-    row8 = row2[:8]
     hc = hcols[...]
     n2_col = nsq[C0 : C0 + STEPS, :]
     n_col = jnp.sqrt(n2_col)
@@ -761,9 +804,9 @@
     ycol = jnp.sum(jnp.where(lane8 == row8, ysol * inv_row, 0.0), axis=1, keepdims=True)
     hy8 = jnp.sum(upper * ysol, axis=1, keepdims=True) * inv_col[:, :1]
     hy9 = jnp.sum(bottom * ysol, axis=1, keepdims=True) / last_n
-    out = guess[...]
+    out = src[K]
     for a in range(K):
-        out = out + rcoef[a : a + 1, :] * rec[a]
+        out = out + rcoef[a : a + 1, :] * src[a]
     res = fields[C0, 0, DEEP : DEEP + X, 0:Y, :]
     for i in range(STEPS):
         ui = fields[C0 + i, 0, DEEP : DEEP + X, 0:Y, :]
@@ -804,7 +847,7 @@
         nflat, ntall = sem_counts(sizes)
         chunks = (NF + CHUNK - 1) // CHUNK
         nsem = ntall + (chunks + 2) * nflat
-        GR = round_up(K + 1, 8)
+        nrecv = 2 * ntall + (2 * chunks + 2) * nflat
         XE, YE = X + 2 * DEEP, Y + 8
         V = lambda *s: pltpu.VMEM(s, jnp.float32)
         vm = pl.BlockSpec(memory_space=pltpu.VMEM)
@@ -820,7 +863,7 @@
         def lanes(d):
             rows, cells = round_up(X * d, 8), d * d
             return [
-                V(2, 1, X, Y, Z), V(2, 2, rows, Z), V(2, 2, 2, cells, Z),
+                V(1, X, Y, Z), V(2, rows, Z), V(2, 2, cells, Z),
                 V(2, 1, X, Y, Z), V(2, 2, 1, d, Y, Z), V(2, 2, rows, Z), V(2, 2, 2, cells, Z),
             ]
 
@@ -828,23 +871,23 @@
         sol, res, hes = pl.pallas_call(
             functools.partial(kernel, sizes, groups),
             out_shape=(shape, shape, jax.ShapeDtypeStruct((STEPS, STEPS + 1), jnp.float32)),
-            in_specs=[vm] * 4,
+            in_specs=[pl.BlockSpec(memory_space=pltpu.HBM)] * 4,
             out_specs=(vm, vm, vm),
             scratch_shapes=[
-                V(NF, X, Y, Z), V(NF, X, Y, Z), V(K, X, Y, Z),
+                V(X, Y, Z), V(X, Y, Z), V(NF, X, Y, Z), V(NF, X, Y, Z), V(K, X, Y, Z),
                 *halo(1), *halo(1), *halo(2), *halo(3), *lanes(1), *lanes(DEEP),
                 V(2, 2, X, Y, Z), V(2, 2, prow, Z), V(2, 2, 2, pcell, Z),
                 V(2, 2, 2, PAIR, Y, Z), V(2, 2, prow, Z), V(2, 2, 2, pcell, Z),
                 V(2, 2, 2, X, Y, Z), V(2, 2, 2, 2, PAIR, Y, Z),
                 V(2, 2, 2, prow, Z), V(2, 2, 2, 2, pcell, Z),
                 V(K + STEPS + 1, 2, XE, YE, Z), V(2, XE, YE, Z), V(2, XE, YE, Z),
-                V(2, XE, YE, Z), V(2, XE, YE, Z), V(2, 2, XE, YE, Z),
-                V(K + 1, GR, Z), V(K, 2 * K, Z),
+                V(2, XE, YE, Z), V(2, XE, YE, Z), V(XE, YE, Z), V(2, 2, XE, YE, Z),
                 V(n_step[0], GF, Z), V(n_step[-1], GF, Z), V(n_step[0], GF, Z), V(n_step[-1], GF, Z),
                 V(2, n_step[0], 1, Z), V(2, n_step[-1], 1, Z),
                 V(32, Z), V(K, Z), V(K, Z), V(K, Z), V(32, Z), V(32, Z), V(32, Z), V(32, Z), V(K, Z),
-                pltpu.SemaphoreType.DMA((nsem,)), pltpu.SemaphoreType.DMA((2, nsem)),
+                pltpu.SemaphoreType.DMA((nsem,)), pltpu.SemaphoreType.DMA((nrecv,)),
                 pltpu.SemaphoreType.DMA((4, len(groups))), pltpu.SemaphoreType.DMA((4, len(groups))),
+                pltpu.SemaphoreType.DMA((4,)),
             ],
             compiler_params=pltpu.CompilerParams(collective_id=0, has_side_effects=True),
         )(right_side, start_guess, conductivity, recycled)

time: 66.3 us -> 61.2 us (0.923)
  Pallas kernels: 65.4 us -> 60.4 us
    pallas_call x1, Pallas kernels: 64 us -> 59 us  [body(): pl.pallas_call(functools.partial(kernel, sizes, groups), out_shape=(shape...]
where the time goes in v3:
time: 61.2 us; the launch traced here: 61 us
  Pallas kernels  60.4 us (99%)
  between operations  0.64 us (1%)
    pallas_call x1, Pallas kernels, body(): pl.pallas_call(functools.partial(kernel, sizes, groups), out_shape=(shape...  59 us
    pallas_call x1, Pallas kernels, body(): pl.pallas_call(deliver, out_shape=(shape, shape, jax.ShapeDtypeStruct(hes...  1.41 us

profile of v3, /device:TPU:0, one launch (start us, length us, event | category | flops | bytes accessed | tf_op | source)
XLA Modules:
  0.0 61.0 jit_solution(17065958920167670076)
XLA Ops:
  0.6 59.0 %shard_map.67 = (f32[4,16,128]{2,1,0:T(8,128)}, f32[4,16,128]{2,1,0:T(8,128)}, f32[8,9]{1,0:T(8,128)}) custom-call(f32[4,16,128]{2,1,0:T(8,128)} %rhs_hbm.1, f32[4,16,128]{2,1,0:T(8,128)} %guess_hbm.1, f32[4,16,128]{2,1,0:T(8,128)} %cond_hbm.1, f32[16,4,16,128]{3,2,1,0:T(8,128)} %rec_hbm.1), custom_call_target="tpu_custom_call" | custom-call | tf_op jit(solution)/shard_map/pallas_call | solution.py:871
  59.6 1.4 %shard_map.68 = (f32[4,16,128]{2,1,0:T(8,128)}, f32[4,16,128]{2,1,0:T(8,128)}, f32[8,9]{1,0:T(8,128)}) custom-call(f32[4,16,128]{2,1,0:T(8,128)} %get-tuple-element.9.sol, f32[4,16,128]{2,1,0:T(8,128)} %get-tuple-element.10.res, f32[8,9]{1,0:T(8,128)} %get-tuple-element.11.hes), custom_call_target="tpu_custom_call" | custom-call | tf_op jit(solution)/shard_map/pallas_call | solution.py:894

commit v4 on v3

--- a/solution.py
+++ b/solution.py
@@ -18,6 +18,8 @@
 DEEP = 3
 PAIR = 2
 VROWS = 24
+VMEM = 67043328
+KEPT = 10310 * 1024
 
 shift_value = 0.4
 SHIFT = 2.8
@@ -51,7 +53,7 @@
     bface3, bedge3, bx3, by3, bc3,
     pack0, pface0, pedge0, zm0, zx0, zy0, zc0,
     pack1, pface1, pedge1, zm1, zx1, zy1, zc1,
-    wbuf, wface, wedge, mx, my, mc, zm2, zx2, zy2, zc2,
+    wbuf, wface, wedge, wpack, wpface, wpedge, mx, my, mc, zm2, zx2, zy2, zc2,
     fields, kext, dext, temp, zext, zw, pe,
     gred1, gred2, nred1, nred2, sred1, sred2,
     mat, na, gmat, n2mat, hcols, nsq, coefa, coefb, ecoef,
@@ -190,7 +192,9 @@
 
     def pair_copies(par):
         def sends(dz):
-            return wbuf.at[par], ends(PAIR), wface.at[par], wedge.at[par]
+            if dz == 0:
+                return wbuf.at[par], ends(PAIR), wface.at[par], wedge.at[par]
+            return wpack.at[par], ends(PAIR), wpface.at[par], wpedge.at[par]
 
         def recvs(h):
             if h is None:
@@ -254,8 +258,14 @@
         for h in range(2):
             place_all(zext.at[h], zm.at[h], zx.at[h], zy.at[h], zc.at[h], 0, depth)
         low = slots(depth)[1]
-        for x in range(DEEP - depth, DEEP + X + depth):
-            zw[x] = jnp.where(low, zext[0, x], zext[1, x])
+        return {
+            x: jnp.where(low, zext[0, x], zext[1, x])
+            for x in range(DEEP - depth, DEEP + X + depth)
+        }
+
+    def keep_zone(planes):
+        for x, v in planes.items():
+            zw[x] = v
 
     def pack_lanes(get, count, depth, pack, pface, pedge):
         lane = lax.broadcasted_iota(jnp.int32, (X, Y, Z), 2)
@@ -418,7 +428,7 @@
             pl.semaphore_signal(barrier, inc=1, device_id=peer, device_id_type=MESH)
         count = count + len(everyone)
 
-    clear_all((wface, wedge, aface, aedge, bface1, bedge1, bface2, bedge2, bface3, bedge3))
+    clear_all((wface, wedge, wpface, wpedge, aface, aedge, bface1, bedge1, bface2, bedge2, bface3, bedge3))
     clear_all((pface0, pedge0, pface1, pedge1))
 
     near_cells = shell_cells(1)
@@ -447,7 +457,7 @@
         ref_rows(src, NF - 1), bface1, bedge1, (NF - 1) * X, NF - 1, (1,), near_cells
     )
     wait_recv(first[NC])
-    fill_zone(1, zm0, zx0, zy0, zc0)
+    keep_zone(fill_zone(1, zm0, zx0, zy0, zc0))
 
     def image(f, carry):
         dst = temp.at[0]
@@ -505,12 +515,13 @@
             pack_edges(ref_rows(img, f), face, edge, f * X, f * len(cells), (s,), cells)
             return carry
 
+        start_halo([c for c in shells[s] if c[0][1] == 0])
         lax.fori_loop(0, NF, pack_shell, 0, unroll=2)
-        start_halo(shells[s])
+        start_halo([c for c in shells[s] if c[0][1] != 0])
 
     for c in second:
         wait_recv(c)
-    fill_zone(DEEP, zm1, zx1, zy1, zc1)
+    keep_zone(fill_zone(DEEP, zm1, zx1, zy1, zc1))
 
     def inner(f, carry):
         fields[f, 0, DEEP : DEEP + X, 0:Y, :] = img[f]
@@ -542,14 +553,22 @@
         va = awf[a]
         return [fold(awf[b] * va) for b in range(a + 1)]
 
-    cross = jnp.concatenate([symmetric(K, K, cross_dots), symmetric(K, K, square_dots)], axis=0)
-    lane_n = lax.broadcasted_iota(jnp.int32, (2 * K, Z), 1)
-    NW = Z // (2 * K // GF)
+    NG = 2
+    NW = Z // (K // NG)
     assert K <= NW
-    part = cross[:GF]
-    for q in range(1, 2 * K // GF):
-        part = part + pltpu.roll(cross[GF * q : GF * q + GF], q * NW, 1)
-    reduce_start(part, (nred1, nred2), 3, 0)
+
+    def squeeze(m):
+        part = m[:NG]
+        for q in range(1, K // NG):
+            part = part + pltpu.roll(m[NG * q : NG * q + NG], q * NW, 1)
+        return part
+
+    def unsqueeze(part):
+        both = [part] + [pltpu.roll(part, Z - q * NW, 1) for q in range(1, K // NG)]
+        lane = lax.broadcasted_iota(jnp.int32, (K, Z), 1)
+        return jnp.where(lane < K, jnp.concatenate(both, axis=0), 0.0)
+
+    reduce_start(squeeze(symmetric(K, K, cross_dots)), (nred1, nred2), 3, 0)
 
     def outer(s, rx, ry, rc):
         wait_recv(shells[s])
@@ -600,13 +619,6 @@
         wait_send(c)
     hcols[...] = jnp.zeros((32, Z), f32)
     nsq[...] = jnp.ones((32, Z), f32)
-
-    def finish_cross():
-        part = reduce_rest((nred1, nred2), 3)
-        both = [part] + [pltpu.roll(part, Z - q * NW, 1) for q in range(1, 2 * K // GF)]
-        both = jnp.where(lane_n < K, jnp.concatenate(both, axis=0), 0.0)
-        na[...] = both[:K]
-        n2mat[...] = both[K:]
 
     def record(j, c1, c2, t1, q1, q2, uu, ww):
         old = hcols[...]
@@ -673,6 +685,10 @@
         bufs = (sred1.at[par], sred2.at[par])
         reduce_start(part, bufs, par, 0)
         if not last:
+            pack_lanes(
+                lambda n: p2 if n else p1, 2, PAIR,
+                wpack.at[par], wpface.at[par], wpedge.at[par],
+            )
             cs = pair_copies(par)
             if j == 0:
                 for s in shells:
@@ -680,23 +696,23 @@
             start_halo(cs)
         if j == 0:
             outer(3, bx3, by3, bc3)
-            finish_cross()
+            na[...] = unsqueeze(reduce_rest((nred1, nred2), 3))
+            n2mat[...] = symmetric(K, K, square_dots)
+        if j == STEPS - 4:
+            reduce_start(squeeze(n2mat[...]), (nred1, nred2), 3, 0)
+        if last:
+            n2mat[...] = unsqueeze(reduce_rest((nred1, nred2), 3))
         for p in pending:
             record(*p)
         if not last:
             wait_recv(cs)
             for n in range(2):
                 place_all(pe.at[n, 0], wbuf.at[par], mx.at[par], my.at[par], mc.at[par], n, PAIR)
-                for h in range(2):
-                    place_all(
-                        zext.at[h], zm2.at[par, h], zx2.at[par, h], zy2.at[par, h],
-                        zc2.at[par, h], n, PAIR,
-                    )
-                for x in range(DEEP - PAIR, DEEP + X + PAIR):
-                    pe[n, 1, x] = jnp.where(
-                        lane_p >= Z - PAIR, zext[0, x],
-                        jnp.where(lane_p < PAIR, zext[1, x], 0.0),
-                    )
+            for x, v in fill_zone(
+                PAIR, zm2.at[par], zx2.at[par], zy2.at[par], zc2.at[par]
+            ).items():
+                for n in range(2):
+                    pe[n, 1, x] = pltpu.roll(v, Z - PAIR - 2 * PAIR * n, 1)
         else:
             pe[1, 0, DEEP : DEEP + X, 0:Y, :] = p2
         total = reduce_rest(bufs, par)
@@ -732,7 +748,7 @@
                 p22 - s * p12 + s * a2e - col_sum(e1 * (2.0 * a3 - n2e)) - col_sum(cc * d_col)
             )
 
-        p_lo, p_n = (DEEP - 1, X + 2) if last else (0, XE)
+        p_lo, p_n = (DEEP - 1, X + 2) if last else (DEEP - PAIR, X + 2 * PAIR)
 
         def combine(p, carry, j=j, p_lo=p_lo):
             z, x = lax.rem(p, 2), p_lo + lax.div(p, 2)
@@ -754,6 +770,16 @@
             fields[C0 + j + 2, z, x] = g
             return carry
 
+        def images_only(p, carry):
+            z, x = lax.rem(p, 2), lax.div(p, 2) * (XE - 1)
+            t = jnp.zeros((YE, Z), f32)
+            for a in range(K):
+                t = t + coefa[a : a + 1, :] * fields[a, z, x]
+            temp[z, x] = t
+            return carry
+
+        if not last:
+            lax.fori_loop(0, 4, images_only, 0, unroll=2)
         lax.fori_loop(0, 2 * p_n, combine, 0, unroll=2)
         w2 = fields.at[C0 + j + 2]
         if last:
@@ -868,6 +894,7 @@
             ]
 
         prow, pcell = round_up(2 * X * PAIR, 8), 2 * PAIR * PAIR
+        lrow, lcell = round_up(X * PAIR, 8), PAIR * PAIR
         sol, res, hes = pl.pallas_call(
             functools.partial(kernel, sizes, groups),
             out_shape=(shape, shape, jax.ShapeDtypeStruct((STEPS, STEPS + 1), jnp.float32)),
@@ -877,25 +904,27 @@
                 V(X, Y, Z), V(X, Y, Z), V(NF, X, Y, Z), V(NF, X, Y, Z), V(K, X, Y, Z),
                 *halo(1), *halo(1), *halo(2), *halo(3), *lanes(1), *lanes(DEEP),
                 V(2, 2, X, Y, Z), V(2, 2, prow, Z), V(2, 2, 2, pcell, Z),
+                V(2, 1, X, Y, Z), V(2, 2, lrow, Z), V(2, 2, 2, lcell, Z),
                 V(2, 2, 2, PAIR, Y, Z), V(2, 2, prow, Z), V(2, 2, 2, pcell, Z),
-                V(2, 2, 2, X, Y, Z), V(2, 2, 2, 2, PAIR, Y, Z),
-                V(2, 2, 2, prow, Z), V(2, 2, 2, 2, pcell, Z),
+                V(2, 2, 1, X, Y, Z), V(2, 2, 2, 1, PAIR, Y, Z),
+                V(2, 2, 2, lrow, Z), V(2, 2, 2, 2, lcell, Z),
                 V(K + STEPS + 1, 2, XE, YE, Z), V(2, XE, YE, Z), V(2, XE, YE, Z),
                 V(2, XE, YE, Z), V(2, XE, YE, Z), V(XE, YE, Z), V(2, 2, XE, YE, Z),
-                V(n_step[0], GF, Z), V(n_step[-1], GF, Z), V(n_step[0], GF, Z), V(n_step[-1], GF, Z),
+                V(n_step[0], GF, Z), V(n_step[-1], GF, Z), V(n_step[0], 2, Z), V(n_step[-1], 2, Z),
                 V(2, n_step[0], 1, Z), V(2, n_step[-1], 1, Z),
                 V(32, Z), V(K, Z), V(K, Z), V(K, Z), V(32, Z), V(32, Z), V(32, Z), V(32, Z), V(K, Z),
                 pltpu.SemaphoreType.DMA((nsem,)), pltpu.SemaphoreType.DMA((nrecv,)),
                 pltpu.SemaphoreType.DMA((4, len(groups))), pltpu.SemaphoreType.DMA((4, len(groups))),
                 pltpu.SemaphoreType.DMA((4,)),
             ],
-            compiler_params=pltpu.CompilerParams(collective_id=0, has_side_effects=True),
+            compiler_params=pltpu.CompilerParams(collective_id=0, has_side_effects=True, vmem_limit_bytes=VMEM - KEPT),
         )(right_side, start_guess, conductivity, recycled)
         sol, res, hes = pl.pallas_call(
             deliver,
             out_shape=(shape, shape, jax.ShapeDtypeStruct(hes.shape, hes.dtype)),
             in_specs=[vm] * 3,
             out_specs=(vm,) * 3,
+            compiler_params=pltpu.CompilerParams(vmem_limit_bytes=8 * 2**20),
         )(sol, res, hes)
         return sol, res, hes.T
 

time: 61.2 us -> 58.9 us (0.962)
  Pallas kernels: 60.4 us -> 58.1 us
    pallas_call x1, Pallas kernels: 59 us -> 57.5 us  [body(): pl.pallas_call(functools.partial(kernel, sizes, groups), out_shape=(shape...]
    pallas_call x1, Pallas kernels: 1.41 us -> 0.63 us  [body(): pl.pallas_call(deliver, out_shape=(shape, shape, jax.ShapeDtypeStruct(hes...]
where the time goes in v4:
time: 58.9 us; the launch traced here: 58.8 us
  Pallas kernels  58.1 us (99%)
  between operations  0.64 us (1%)
    pallas_call x1, Pallas kernels, body(): pl.pallas_call(functools.partial(kernel, sizes, groups), out_shape=(shape...  57.5 us

profile of v4, /device:TPU:0, one launch (start us, length us, event | category | flops | bytes accessed | tf_op | source)
XLA Modules:
  0.0 58.8 jit_solution(15935124186426786433)
XLA Ops:
  0.6 57.5 %shard_map.67 = (f32[4,16,128]{2,1,0:T(8,128)S(1)}, f32[4,16,128]{2,1,0:T(8,128)S(1)}, f32[8,9]{1,0:T(8,128)S(1)}) custom-call(f32[4,16,128]{2,1,0:T(8,128)} %rhs_hbm.1, f32[4,16,128]{2,1,0:T(8,128)} %guess_hbm.1, f32[4,16,128]{2,1,0:T(8,128)} %cond_hbm.1, f32[16,4,16,128]{3,2,1,0:T(8,128)} %rec_hbm.1), custom_call_target="tpu_custom_call" | custom-call | tf_op jit(solution)/shard_map/pallas_call | solution.py:898
  58.1 0.6 %shard_map.68 = (f32[4,16,128]{2,1,0:T(8,128)}, f32[4,16,128]{2,1,0:T(8,128)}, f32[8,9]{1,0:T(8,128)}) custom-call(f32[4,16,128]{2,1,0:T(8,128)S(1)} %get-tuple-element.9.sol, f32[4,16,128]{2,1,0:T(8,128)S(1)} %get-tuple-element.10.res, f32[8,9]{1,0:T(8,128)S(1)} %get-tuple-element.11.hes), custom_call_target="tpu_custom_call" | custom-call | tf_op jit(solution)/shard_map/pallas_call | solution.py:922

commit v5 on v4

--- a/solution.py
+++ b/solution.py
@@ -813,18 +813,27 @@
         picked = jnp.where(lane_t == row_t, hes[:, col : col + 1], 0.0)
         hes_out[col : col + 1, :] = jnp.sum(picked, axis=0, keepdims=True)[:, : STEPS + 1]
 
-    rows = [hes[i : i + 1] for i in range(STEPS + 1)]
-    rows[0] = jnp.where(lane1 == STEPS, n_col[0:1], rows[0])
+    h = {
+        (r, c): jnp.broadcast_to(hes[r : r + 1, c : c + 1], (1, Z))
+        for c in range(STEPS) for r in range(c + 2)
+    }
+    goal = [n_col[0:1]] + [jnp.zeros((1, Z), f32)] * STEPS
     for i in range(STEPS):
-        top, low = rows[i][:, i : i + 1], rows[i + 1][:, i : i + 1]
+        top, low = h[i, i], h[i + 1, i]
         inv_r = 1.0 / jnp.sqrt(top * top + low * low)
         cs_, sn = top * inv_r, low * inv_r
-        rows[i], rows[i + 1] = cs_ * rows[i] + sn * rows[i + 1], cs_ * rows[i + 1] - sn * rows[i]
+        for c in range(i, STEPS):
+            up, down = h[i, c], h[i + 1, c]
+            h[i, c], h[i + 1, c] = cs_ * up + sn * down, cs_ * down - sn * up
+        goal[i], goal[i + 1] = cs_ * goal[i] + sn * goal[i + 1], cs_ * goal[i + 1] - sn * goal[i]
+    found = {}
     ysol = jnp.zeros((1, Z), f32)
     for i in range(STEPS - 1, -1, -1):
-        known = jnp.sum(jnp.where(lane1 > i, rows[i] * ysol, 0.0), axis=1, keepdims=True)
-        yi = (rows[i][:, STEPS : STEPS + 1] - known) / rows[i][:, i : i + 1]
-        ysol = jnp.where(lane1 == i, yi, ysol)
+        rest = goal[i]
+        for c in range(STEPS - 1, i, -1):
+            rest = rest - h[i, c] * found[c]
+        found[i] = rest * (1.0 / h[i, i])
+        ysol = jnp.where(lane1 == i, found[i], ysol)
 
     rcoef = ecoef[:, :1] - jnp.sum(hc[:K] * (ysol * inv_row), axis=1, keepdims=True)
     ycol = jnp.sum(jnp.where(lane8 == row8, ysol * inv_row, 0.0), axis=1, keepdims=True)

time: 58.9 us -> 57.3 us (0.973)
  Pallas kernels: 58.1 us -> 56.5 us
    pallas_call x1, Pallas kernels: 57.5 us -> 55.9 us  [body(): pl.pallas_call(functools.partial(kernel, sizes, groups), out_shape=(shape...]
where the time goes in v5:
time: 57.3 us; the launch traced here: 57.2 us
  Pallas kernels  56.5 us (99%)
  between operations  0.64 us (1%)
    pallas_call x1, Pallas kernels, body(): pl.pallas_call(functools.partial(kernel, sizes, groups), out_shape=(shape...  55.9 us

profile of v5, /device:TPU:0, one launch (start us, length us, event | category | flops | bytes accessed | tf_op | source)
XLA Modules:
  0.0 57.2 jit_solution(17325503489190001323)
XLA Ops:
  0.6 55.9 %shard_map.67 = (f32[4,16,128]{2,1,0:T(8,128)S(1)}, f32[4,16,128]{2,1,0:T(8,128)S(1)}, f32[8,9]{1,0:T(8,128)S(1)}) custom-call(f32[4,16,128]{2,1,0:T(8,128)} %rhs_hbm.1, f32[4,16,128]{2,1,0:T(8,128)} %guess_hbm.1, f32[4,16,128]{2,1,0:T(8,128)} %cond_hbm.1, f32[16,4,16,128]{3,2,1,0:T(8,128)} %rec_hbm.1), custom_call_target="tpu_custom_call" | custom-call | tf_op jit(solution)/shard_map/pallas_call | solution.py:907
  56.5 0.6 %shard_map.68 = (f32[4,16,128]{2,1,0:T(8,128)}, f32[4,16,128]{2,1,0:T(8,128)}, f32[8,9]{1,0:T(8,128)}) custom-call(f32[4,16,128]{2,1,0:T(8,128)S(1)} %get-tuple-element.9.sol, f32[4,16,128]{2,1,0:T(8,128)S(1)} %get-tuple-element.10.res, f32[8,9]{1,0:T(8,128)S(1)} %get-tuple-element.11.hes), custom_call_target="tpu_custom_call" | custom-call | tf_op jit(solution)/shard_map/pallas_call | solution.py:931

commit v6 on v5

--- a/solution.py
+++ b/solution.py
@@ -658,14 +658,6 @@
         p1 = p1r[0, DEEP : DEEP + X, 0:Y, :]
         p2 = wbuf[par, 1]
         wbuf[par, 0] = p1
-        if not last:
-            for n, v in ((0, p1), (1, p2)):
-                cells = square_cells(PAIR)
-                pack_edges(
-                    value_rows(v), wface.at[par], wedge.at[par], n * X * PAIR,
-                    n * len(cells), tuple(range(1, PAIR + 1)), cells,
-                )
-
         rows1, rows2 = [], []
         for f in range(K + j + 1):
             v = fields[f, 0, DEEP : DEEP + X, 0:Y, :]
@@ -685,6 +677,12 @@
         bufs = (sred1.at[par], sred2.at[par])
         reduce_start(part, bufs, par, 0)
         if not last:
+            for n, v in ((0, p1), (1, p2)):
+                cells = square_cells(PAIR)
+                pack_edges(
+                    value_rows(v), wface.at[par], wedge.at[par], n * X * PAIR,
+                    n * len(cells), tuple(range(1, PAIR + 1)), cells,
+                )
             pack_lanes(
                 lambda n: p2 if n else p1, 2, PAIR,
                 wpack.at[par], wpface.at[par], wpedge.at[par],

time: 57.3 us -> 57.3 us (level)
  no operation moved by 1% of the time
where the time goes in v6:
time: 57.3 us; the launch traced here: 57.2 us
  Pallas kernels  56.5 us (99%)
  between operations  0.64 us (1%)
    pallas_call x1, Pallas kernels, body(): pl.pallas_call(functools.partial(kernel, sizes, groups), out_shape=(shape...  55.9 us

profile of v6, /device:TPU:0, one launch (start us, length us, event | category | flops | bytes accessed | tf_op | source)
XLA Modules:
  0.0 57.2 jit_solution(5289430590898367265)
XLA Ops:
  0.6 55.9 %shard_map.67 = (f32[4,16,128]{2,1,0:T(8,128)S(1)}, f32[4,16,128]{2,1,0:T(8,128)S(1)}, f32[8,9]{1,0:T(8,128)S(1)}) custom-call(f32[4,16,128]{2,1,0:T(8,128)} %rhs_hbm.1, f32[4,16,128]{2,1,0:T(8,128)} %guess_hbm.1, f32[4,16,128]{2,1,0:T(8,128)} %cond_hbm.1, f32[16,4,16,128]{3,2,1,0:T(8,128)} %rec_hbm.1), custom_call_target="tpu_custom_call" | custom-call | tf_op jit(solution)/shard_map/pallas_call | solution.py:905
  56.5 0.6 %shard_map.68 = (f32[4,16,128]{2,1,0:T(8,128)}, f32[4,16,128]{2,1,0:T(8,128)}, f32[8,9]{1,0:T(8,128)}) custom-call(f32[4,16,128]{2,1,0:T(8,128)S(1)} %get-tuple-element.9.sol, f32[4,16,128]{2,1,0:T(8,128)S(1)} %get-tuple-element.10.res, f32[8,9]{1,0:T(8,128)S(1)} %get-tuple-element.11.hes), custom_call_target="tpu_custom_call" | custom-call | tf_op jit(solution)/shard_map/pallas_call | solution.py:929
